TPU v7x, 32 devices: a whole 2x2x4 slice. The times are simulated.
32 devices in a mesh: dp: 8 (over z, x), tensor: 4 (over y, core).
Axes of the slice: x: 2, y: 2, z: 4, core: 2. Of those that a mesh axis runs over, the one named last changes fastest.
Arguments:
- latents: bfloat16 [8, 1056, 1536], P('dp', 'tensor'), may hold values from -6 to 6
- context: bfloat16 [8, 130, 1536], P('dp'), may hold values from -6 to 6
- lengths: int32 [8], P('dp'), may hold values from 769 to 1025, as said below
- cotangent: bfloat16 [8, 1056, 1536], P('dp', 'tensor'), may hold values from -6 to 6
- attn_weights: bfloat16 [8, 1536, 1536], P(None, 'dp', 'tensor')
- mlp_weights: bfloat16 [3, 1536, 6144], P(None, 'dp', 'tensor')
- norm_gains: bfloat16 [3, 1536], P(None, 'dp'), may hold values from 0.5 to 1.5
- attn_momenta: float32 [8, 1536, 1536], P(None, 'dp', 'tensor')
- mlp_momenta: float32 [3, 1536, 6144], P(None, 'dp', 'tensor')
- gain_momenta: float32 [3, 1536], P(None, 'dp'), may hold values from -256 to 256
Outputs:
- output: bfloat16 [8, 1056, 1536], P('dp', 'tensor')
- latent_grad: float32 [8, 1056, 1536], P('dp', 'tensor')
- context_grad: float32 [8, 130, 1536], P('dp', None, 'tensor')
- attn_grad: float32 [8, 1536, 1536], P(None, 'dp', 'tensor')
- mlp_grad: float32 [3, 1536, 6144], P(None, 'dp', 'tensor')
- gain_grad: float32 [3, 1536], P(None, 'dp')
- attn_moment: float32 [8, 1536, 1536], P(None, 'dp', 'tensor')
- mlp_moment: float32 [3, 1536, 6144], P(None, 'dp', 'tensor')
- gain_moment: float32 [3, 1536], P(None, 'dp')
- attn_step: float32 [8, 1536, 1536], P(None, 'dp', 'tensor')
- mlp_step: float32 [3, 1536, 6144], P(None, 'dp', 'tensor')
- gain_step: float32 [3, 1536], P(None, 'dp')
Inputs may be any that keep to these rules, and one draw needn't show every extreme that they name: `lengths`: keys at slots at or beyond a sequence's length are ignored; some sequence has exactly 1025.
All inputs are finite; a program needn't handle non-finite values.
Results may differ from a plain program's by a relative error of at most 0.025.
Values may be sent and summed in bfloat16 or wider, within the bound.
A program may use at most 256 MiB of HBM per device.

v0:
```python
import math

import jax
import jax.numpy as jnp
from jax import lax
from jax.sharding import PartitionSpec as P

D = 1536
HD = 64
FF = 6144
NS_ITERS = 2


highest = lax.Precision.HIGHEST
ns_linear = 3.4445
ns_cubic = -4.775
ns_quintic = 2.0315
muon_rate = 0.2
gain_rate = 0.001
norm_epsilon = 1e-05
muon_epsilon = 1e-07


def layer_norm(value_rows, gain):
    center = value_rows - jnp.mean(value_rows, axis=-1, keepdims=True)
    spread = jnp.mean(center * center, axis=-1, keepdims=True)
    return center * lax.rsqrt(spread + norm_epsilon) * gain


def rotate(value_rows, direction):
    pair_count = HD // 4
    inverse = jnp.exp(jnp.arange(pair_count, dtype=jnp.float32) * (-math.log(10000.0) / pair_count))
    positions = jnp.arange(value_rows.shape[1], dtype=jnp.float32)
    angles = positions[:, None] * inverse[None, :]
    cosine = jnp.cos(angles)[None, :, None, :]
    sine_part = direction * jnp.sin(angles)[None, :, None, :]
    leading = value_rows[..., :pair_count]
    trailing = value_rows[..., pair_count : 2 * pair_count]
    untouched = value_rows[..., 2 * pair_count :]
    return jnp.concatenate(
        [
            leading * cosine - trailing * sine_part,
            trailing * cosine + leading * sine_part,
            untouched,
        ],
        axis=-1,
    )


def attend_forward(query, keys, value, length):
    scores = jnp.einsum("ihd,jhd->hij", query, keys, preferred_element_type=jnp.float32)
    usable = jnp.arange(keys.shape[0], dtype=jnp.int32) < length
    scaled = jnp.where(usable[None, None, :], scores * 0.125, -1000000000.0)
    biggest = jnp.max(scaled, axis=-1, keepdims=True)
    logsum = biggest + jnp.log(jnp.sum(jnp.exp(scaled - biggest), axis=-1, keepdims=True))
    weights = jnp.exp(scaled - logsum).astype(jnp.bfloat16)
    output = jnp.einsum("hij,jhd->ihd", weights, value, preferred_element_type=jnp.float32)
    return (output.astype(jnp.bfloat16), logsum)


def attend_backward(query, keys, value, grad_output, logsum, length):
    scores = jnp.einsum("ihd,jhd->hij", query, keys, preferred_element_type=jnp.float32)
    usable = jnp.arange(keys.shape[0], dtype=jnp.int32) < length
    scaled = jnp.where(usable[None, None, :], scores * 0.125, -1000000000.0)
    probs = jnp.exp(scaled - logsum)
    grad_probs = jnp.einsum("ihd,jhd->hij", grad_output, value, preferred_element_type=jnp.float32)
    grad_value = jnp.einsum(
        "hij,ihd->jhd", probs.astype(jnp.bfloat16), grad_output, preferred_element_type=jnp.float32
    )
    totals = jnp.sum(probs * grad_probs, axis=-1, keepdims=True)
    grad_scores = (probs * (grad_probs - totals) * 0.125).astype(jnp.bfloat16)
    grad_query = jnp.einsum("hij,jhd->ihd", grad_scores, keys, preferred_element_type=jnp.float32)
    grad_keys = jnp.einsum("hij,ihd->jhd", grad_scores, query, preferred_element_type=jnp.float32)
    return (grad_query, grad_keys, grad_value)


def project(value_rows, weight_matrix):
    return jnp.einsum("acz,zy->acy", value_rows, weight_matrix, preferred_element_type=jnp.float32)


def expand(value_rows, weight_matrix):
    return jnp.einsum("xby,ay->xba", value_rows, weight_matrix, preferred_element_type=jnp.float32)


def outer(gradient_tree, value_rows):
    return jnp.einsum("mgf,mgx->xf", gradient_tree, value_rows, preferred_element_type=jnp.float32)


def shards(
    latents,
    context,
    lengths,
    cotangent,
    attn_weights,
    mlp_weights,
    norm_gains,
    attn_momenta,
    mlp_momenta,
    gain_momenta,
):
    seq_count = latents.shape[0]
    inner = attn_weights.shape[2]
    head_local = inner // HD

    def split_heads(value_rows):
        return value_rows.reshape(value_rows.shape[0], value_rows.shape[1], head_local, HD)

    def merge_heads(value_rows):
        return value_rows.reshape(value_rows.shape[0], value_rows.shape[1], inner)

    def spread_rows(value_rows):
        return lax.all_gather(value_rows, "tensor", axis=1, tiled=True)

    def collect_rows(value_rows):
        return lax.psum_scatter(value_rows, "tensor", scatter_dimension=1, tiled=True)

    def spread_grads(value_rows):
        return lax.all_gather(value_rows, "tensor", axis=1, tiled=True)

    def collect_grads(value_rows):
        return lax.psum_scatter(
            value_rows.astype(jnp.bfloat16), "tensor", scatter_dimension=1, tiled=True
        ).astype(jnp.float32)

    def forward_map(query, keys, value, length_list):
        return lax.map(
            lambda packed: attend_forward(packed[0], packed[1], packed[2], packed[3]),
            (query, keys, value, length_list),
        )

    def backward_map(query, keys, value, grad_output, logsum, length_list):
        return lax.map(
            lambda packed: attend_backward(
                packed[0], packed[1], packed[2], packed[3], packed[4], packed[5]
            ),
            (query, keys, value, grad_output, logsum, length_list),
        )

    attn_full, mlp_full, gain_full = (
        lax.all_gather(attn_weights, "dp", axis=1, tiled=True),
        lax.all_gather(mlp_weights, "dp", axis=1, tiled=True),
        lax.all_gather(norm_gains, "dp", axis=1, tiled=True),
    )
    gain_values = gain_full.astype(jnp.float32)
    resid_zero = latents.astype(jnp.float32)
    rows_one = spread_rows(layer_norm(resid_zero, gain_values[0]).astype(jnp.bfloat16))
    query_self = rotate(split_heads(project(rows_one, attn_full[0])), 1.0).astype(jnp.bfloat16)
    keys_self = rotate(split_heads(project(rows_one, attn_full[1])), 1.0).astype(jnp.bfloat16)
    value_self = split_heads(project(rows_one, attn_full[2]).astype(jnp.bfloat16))
    attended, logsum_self = forward_map(query_self, keys_self, value_self, lengths)
    attended = merge_heads(attended)
    resid_one = resid_zero + collect_rows(expand(attended, attn_full[3]))
    rows_two = spread_rows(layer_norm(resid_one, gain_values[1]).astype(jnp.bfloat16))
    query_cross = split_heads(project(rows_two, attn_full[4]).astype(jnp.bfloat16))
    keys_cross = split_heads(project(context, attn_full[5]).astype(jnp.bfloat16))
    value_cross = split_heads(project(context, attn_full[6]).astype(jnp.bfloat16))
    cond_lengths = jnp.full((seq_count,), keys_cross.shape[1], jnp.int32)
    crossed, logsum_cross = forward_map(query_cross, keys_cross, value_cross, cond_lengths)
    crossed = merge_heads(crossed)
    resid_two = resid_one + collect_rows(expand(crossed, attn_full[7]))
    rows_three = spread_rows(layer_norm(resid_two, gain_values[2]).astype(jnp.bfloat16))
    gate = project(rows_three, mlp_full[0])
    upward = project(rows_three, mlp_full[1])
    hidden_state = (jax.nn.silu(gate) * upward).astype(jnp.bfloat16)
    result = (resid_two + collect_rows(expand(hidden_state, mlp_full[2]))).astype(jnp.bfloat16)
    attn_back, perceptron_backward, gain_back = (
        lax.all_gather(attn_weights, "dp", axis=1, tiled=True),
        lax.all_gather(mlp_weights, "dp", axis=1, tiled=True),
        lax.all_gather(norm_gains, "dp", axis=1, tiled=True),
    )
    gain_back = gain_back.astype(jnp.float32)
    gradient_mixture = spread_grads(cotangent)
    grad_hidden = jnp.einsum(
        "zpc,cx->zpx", gradient_mixture, perceptron_backward[2], preferred_element_type=jnp.float32
    )
    down_weight = jnp.einsum(
        "moj,mor->rj", hidden_state, gradient_mixture, preferred_element_type=jnp.float32
    )
    unused_value, gate_pull = jax.vjp(
        lambda gate_in, up_in: jax.nn.silu(gate_in) * up_in, gate, upward
    )
    grad_gate, grad_up = gate_pull(grad_hidden)
    grad_gate = grad_gate.astype(jnp.bfloat16)
    grad_up = grad_up.astype(jnp.bfloat16)
    weight_gate = outer(grad_gate, rows_three)
    weight_up = outer(grad_up, rows_three)
    normed_three_grad = collect_grads(
        expand(grad_gate, perceptron_backward[0]) + expand(grad_up, perceptron_backward[1])
    )
    unused_norm, norm_pull = jax.vjp(layer_norm, resid_two, gain_back[2])
    resid_grad, gain_three = norm_pull(normed_three_grad)
    grad_two = cotangent.astype(jnp.float32) + resid_grad
    grad_cross_out = spread_grads(grad_two.astype(jnp.bfloat16))
    weight_cross_out = outer(crossed, grad_cross_out)
    grad_crossed = split_heads(project(grad_cross_out, attn_back[7]).astype(jnp.bfloat16))
    grad_q_cross, grad_k_cross, grad_v_cross = backward_map(
        query_cross, keys_cross, value_cross, grad_crossed, logsum_cross, cond_lengths
    )
    grad_q_cross = merge_heads(grad_q_cross.astype(jnp.bfloat16))
    grad_k_cross = merge_heads(grad_k_cross.astype(jnp.bfloat16))
    grad_v_cross = merge_heads(grad_v_cross.astype(jnp.bfloat16))
    weight_q_cross = outer(grad_q_cross, rows_two)
    weight_k_cross = outer(grad_k_cross, context)
    weight_v_cross = outer(grad_v_cross, context)
    cond_partial = expand(grad_k_cross, attn_back[5]) + expand(grad_v_cross, attn_back[6])
    normed_two_grad, context_grad = (
        lax.psum_scatter(
            expand(grad_q_cross, attn_back[4]).astype(jnp.bfloat16),
            "tensor",
            scatter_dimension=1,
            tiled=True,
        ).astype(jnp.float32),
        lax.psum_scatter(
            cond_partial.astype(jnp.bfloat16), "tensor", scatter_dimension=2, tiled=True
        ).astype(jnp.float32),
    )
    unused_norm, norm_pull = jax.vjp(layer_norm, resid_one, gain_back[1])
    resid_grad, gain_two = norm_pull(normed_two_grad)
    grad_one = grad_two + resid_grad
    grad_self_out = spread_grads(grad_one.astype(jnp.bfloat16))
    weight_self_out = outer(attended, grad_self_out)
    grad_attended = split_heads(project(grad_self_out, attn_back[3]).astype(jnp.bfloat16))
    grad_q_self, grad_k_self, grad_v_self = backward_map(
        query_self, keys_self, value_self, grad_attended, logsum_self, lengths
    )
    grad_q_self = merge_heads(rotate(grad_q_self, -1.0).astype(jnp.bfloat16))
    grad_k_self = merge_heads(rotate(grad_k_self, -1.0).astype(jnp.bfloat16))
    grad_v_self = merge_heads(grad_v_self.astype(jnp.bfloat16))
    weight_query = outer(grad_q_self, rows_one)
    weight_keys = outer(grad_k_self, rows_one)
    weight_value = outer(grad_v_self, rows_one)
    normed_one_grad = collect_grads(
        expand(grad_q_self, attn_back[0])
        + expand(grad_k_self, attn_back[1])
        + expand(grad_v_self, attn_back[2])
    )
    unused_norm, norm_pull = jax.vjp(layer_norm, resid_zero, gain_back[0])
    resid_grad, gain_one = norm_pull(normed_one_grad)
    latent_grad = grad_one + resid_grad
    attn_terms = jnp.stack(
        [
            weight_query,
            weight_keys,
            weight_value,
            weight_self_out,
            weight_q_cross,
            weight_k_cross,
            weight_v_cross,
            weight_cross_out,
        ]
    )
    mlp_terms = jnp.stack([weight_gate, weight_up, down_weight])
    gain_terms = jnp.stack([gain_one, gain_two, gain_three])
    attn_grad, mlp_grad, gain_part = (
        lax.psum_scatter(
            attn_terms.astype(jnp.bfloat16), "dp", scatter_dimension=1, tiled=True
        ).astype(jnp.float32),
        lax.psum_scatter(
            mlp_terms.astype(jnp.bfloat16), "dp", scatter_dimension=1, tiled=True
        ).astype(jnp.float32),
        lax.psum_scatter(
            gain_terms.astype(jnp.bfloat16), "dp", scatter_dimension=1, tiled=True
        ).astype(jnp.float32),
    )
    attn_moment = 0.5 * attn_momenta + 0.5 * attn_grad
    mlp_moment = 0.5 * mlp_momenta + 0.5 * mlp_grad
    total_attn, total_mlp = lax.psum(
        (
            jnp.sum(attn_moment * attn_moment, axis=(1, 2)),
            jnp.sum(mlp_moment * mlp_moment, axis=(1, 2)),
        ),
        ("dp", "tensor"),
    )
    local_attn = attn_moment / (jnp.sqrt(total_attn) + muon_epsilon)[:, None, None]
    local_mlp = mlp_moment / (jnp.sqrt(total_mlp) + muon_epsilon)[:, None, None]
    gain_grad = gain_part
    for iteration in range(NS_ITERS):
        whole_attn, whole_mlp = (
            lax.all_gather(local_attn.astype(jnp.bfloat16), "dp", axis=1, tiled=True).astype(
                local_attn.dtype
            ),
            lax.all_gather(local_mlp.astype(jnp.bfloat16), "dp", axis=1, tiled=True).astype(
                local_mlp.dtype
            ),
        )
        part_attn = jnp.einsum(
            "mdr,mcr->mdc",
            whole_attn,
            local_attn,
            precision=highest,
            preferred_element_type=jnp.float32,
        )
        part_mlp = jnp.einsum(
            "mdr,mcr->mdc",
            whole_mlp,
            local_mlp,
            precision=highest,
            preferred_element_type=jnp.float32,
        )
        if iteration == 0:
            gram_attn, gram_mlp, gain_grad = (
                lax.psum(part_attn.astype(jnp.bfloat16), "tensor").astype(jnp.float32),
                lax.psum(part_mlp.astype(jnp.bfloat16), "tensor").astype(jnp.float32),
                lax.psum(gain_part.astype(jnp.bfloat16), "tensor").astype(jnp.float32),
            )
        else:
            gram_attn, gram_mlp = (
                lax.psum(part_attn.astype(jnp.bfloat16), "tensor").astype(jnp.float32),
                lax.psum(part_mlp.astype(jnp.bfloat16), "tensor").astype(jnp.float32),
            )
        single_attn = jnp.einsum(
            "mdc,mdr->mcr",
            gram_attn,
            whole_attn,
            precision=highest,
            preferred_element_type=jnp.float32,
        )
        single_mlp = jnp.einsum(
            "mdc,mdr->mcr",
            gram_mlp,
            whole_mlp,
            precision=highest,
            preferred_element_type=jnp.float32,
        )
        square_attn, square_mlp = (
            lax.psum(
                jnp.einsum(
                    "mdr,mcr->mdc",
                    whole_attn,
                    single_attn,
                    precision=highest,
                    preferred_element_type=jnp.float32,
                ).astype(jnp.bfloat16),
                "tensor",
            ).astype(jnp.float32),
            lax.psum(
                jnp.einsum(
                    "mdr,mcr->mdc",
                    whole_mlp,
                    single_mlp,
                    precision=highest,
                    preferred_element_type=jnp.float32,
                ).astype(jnp.bfloat16),
                "tensor",
            ).astype(jnp.float32),
        )
        double_attn = jnp.einsum(
            "mdc,mdr->mcr",
            square_attn,
            whole_attn,
            precision=highest,
            preferred_element_type=jnp.float32,
        )
        double_mlp = jnp.einsum(
            "mdc,mdr->mcr",
            square_mlp,
            whole_mlp,
            precision=highest,
            preferred_element_type=jnp.float32,
        )
        local_attn = ns_linear * local_attn + ns_cubic * single_attn + ns_quintic * double_attn
        local_mlp = ns_linear * local_mlp + ns_cubic * single_mlp + ns_quintic * double_mlp
    attn_step = -muon_rate * local_attn
    mlp_step = -muon_rate * max(1.0, FF / D) ** 0.5 * local_mlp
    gain_moment = 0.5 * gain_momenta + 0.5 * gain_grad
    gain_step = -gain_rate * gain_moment
    return (
        result,
        latent_grad,
        context_grad,
        attn_grad,
        mlp_grad,
        gain_grad,
        attn_moment,
        mlp_moment,
        gain_moment,
        attn_step,
        mlp_step,
        gain_step,
    )


def solution(mesh):
    in_specs = (
        P("dp", "tensor", None),
        P("dp", None, None),
        P("dp"),
        P("dp", "tensor", None),
        P(None, "dp", "tensor"),
        P(None, "dp", "tensor"),
        P(None, "dp"),
        P(None, "dp", "tensor"),
        P(None, "dp", "tensor"),
        P(None, "dp"),
    )
    out_specs = (
        P("dp", "tensor", None),
        P("dp", "tensor", None),
        P("dp", None, "tensor"),
        P(None, "dp", "tensor"),
        P(None, "dp", "tensor"),
        P(None, "dp"),
        P(None, "dp", "tensor"),
        P(None, "dp", "tensor"),
        P(None, "dp"),
        P(None, "dp", "tensor"),
        P(None, "dp", "tensor"),
        P(None, "dp"),
    )
    return jax.shard_map(shards, mesh=mesh, in_specs=in_specs, out_specs=out_specs, check_vma=False)
```

profile of v0, /device:TPU:26, one launch (start us, length us, event | category | flops | bytes accessed | tf_op | source)
XLA Modules:
  0.0 2793.5 jit_solution(10718919368811791616)
XLA Ops:
  7.2 24.8 all-gather
  41.0 27.7 all-gather.14.cloned.1.call-done
  68.8 136.6 %all-gather.16.cloned.1.call-done = bf16[8,1536,384]{2,1,0:T(8,128)(2,1)} async-done(((bf16[8,192,384]{2,1,0:T(8,128)(2,1)}), bf16[8,1536,384]{2,1,0:T(8,128)(2,1)}) %all-gather.16.cloned.1.call-update) | async-done | bytes 9437200 | tf_op jit(solution)/shard_map/all_gather | solution.py:140
  266.7 61.3 %reduce-scatter.15.cloned.1.call-done = f32[1,264,1536]{2,1,0:T(8,128)} async-done(((f32[1,1056,1536]{2,1,0:T(8,128)}), f32[1,264,1536]{2,1,0:T(8,128)}) %reduce-scatter.15.cloned.1.call-update) | async-done | bytes 1622032 | tf_op jit(solution)/shard_map/reduce_scatter | solution.py:115
  335.0 25.5 all-gather.18.cloned.1.call-done
  376.7 59.7 %reduce-scatter.17.cloned.1.call-done = f32[1,264,1536]{2,1,0:T(8,128)} async-done(((f32[1,1056,1536]{2,1,0:T(8,128)}), f32[1,264,1536]{2,1,0:T(8,128)}) %reduce-scatter.17.cloned.1.call-update) | async-done | bytes 1622032 | tf_op jit(solution)/shard_map/reduce_scatter | solution.py:115
  441.4 189.5 %all-gather.22.cloned.1.call-done = bf16[3,1536,1536]{2,1,0:T(8,128)(2,1)} async-done(((bf16[3,192,1536]{2,1,0:T(8,128)(2,1)}), bf16[3,1536,1536]{2,1,0:T(8,128)(2,1)}) %all-gather.22.cloned.1.call-update) | async-done | bytes 14155792 | tf_op jit(solution)/shard_map/all_gather | solution.py:141
  630.9 32.3 %all-gather.20.cloned.1.call-done = bf16[1,1056,1536]{2,1,0:T(8,128)(2,1)} async-done(((bf16[1,264,1536]{2,1,0:T(8,128)(2,1)}), bf16[1,1056,1536]{2,1,0:T(8,128)(2,1)}) %all-gather.20.cloned.1.call-update) | async-done | bytes 3244048 | tf_op jit(solution)/shard_map/all_gather | solution.py:112
  735.9 28.5 %reduce-scatter.21.cloned.1.call-done = bf16[1,264,1536]{2,1,0:T(8,128)(2,1)} async-done(((bf16[1,1056,1536]{2,1,0:T(8,128)(2,1)}), bf16[1,264,1536]{2,1,0:T(8,128)(2,1)}) %reduce-scatter.21.cloned.1.call-update) | async-done | bytes 811024 | tf_op jit(solution)/shard_map/reduce_scatter | solution.py:121
  767.3 59.7 %reduce-scatter.19.cloned.1.call-done = f32[1,264,1536]{2,1,0:T(8,128)} async-done(((f32[1,1056,1536]{2,1,0:T(8,128)}), f32[1,264,1536]{2,1,0:T(8,128)}) %reduce-scatter.19.cloned.1.call-update) | async-done | bytes 1622032 | tf_op jit(solution)/shard_map/reduce_scatter | solution.py:115
  833.0 29.2 %all-gather.26.cloned.1.call-done = bf16[1,1056,1536]{2,1,0:T(8,128)(2,1)} async-done(((bf16[1,264,1536]{2,1,0:T(8,128)(2,1)}), bf16[1,1056,1536]{2,1,0:T(8,128)(2,1)}) %all-gather.26.cloned.1.call-update) | async-done | bytes 3244048 | tf_op jit(solution)/shard_map/all_gather | solution.py:118
  884.7 38.6 %reduce-scatter.23.cloned.1.call-done = bf16[1,264,1536]{2,1,0:T(8,128)(2,1)} async-done(((bf16[1,1056,1536]{2,1,0:T(8,128)(2,1)}), bf16[1,264,1536]{2,1,0:T(8,128)(2,1)}) %reduce-scatter.23.cloned.1.call-update) | async-done | bytes 811024 | tf_op jit(solution)/shard_map/reduce_scatter | solution.py:207
  977.5 30.1 %fusion.86 = f32[1,1056,6,64]{1,3,2,0:T(8,128)} fusion(f32[6,1056,1056]{1,2,0:T(8,128)} %get-tuple-element.213, f32[6,1056]{1,0:T(8,128)S(1)} %copy-done.36, bf16[1056,6,64]{0,2,1:T(8,128)(2,1)S(1)} %bitcast.370, bf16[1056,6,64]{0,2,1:T(8,128)(2,1)S(1)} %bitcast.366, bf16[1056,6,32]{0,2,1:T(8,128)(2,1)S(1)} %copy-done.34, ...), kind=kOutput, calls=%fused_computation.107 | convolution fusion | flops 2618549504 | bytes 30843648 | tf_op jit(solution)/shard_map/while/body/eval_jaxpr/hij,jhd->ihd/dot_general | solution.py:72
  1008.8 31.5 %fusion.91 = f32[1,1056,6,64]{1,3,2,0:T(8,128)} fusion(f32[6,1056,1056]{1,2,0:T(8,128)} %get-tuple-element.213, f32[6,1056]{1,0:T(8,128)S(1)} %copy-done.36, bf16[1056,6,64]{0,2,1:T(8,128)(2,1)S(1)} %bitcast.371, bf16[1056,6,64]{0,2,1:T(8,128)(2,1)S(1)} %bitcast.367, bf16[1056,6,32]{0,2,1:T(8,128)(2,1)} %copy-done.32, bf16[1056,6,16]{0,2,1:T(8,128)(2,1)} %copy-done.40, ...), kind=kOutput, calls=%fused_computation.108 | convolution fusion | flops 2618549504 | bytes 30843648 | tf_op jit(solution)/shard_map/while/body/eval_jaxpr/hij,ihd->jhd/dot_general | solution.py:73
  1079.2 110.9 %reduce-scatter.29.cloned.1.call-done = bf16[3,192,1536]{2,1,0:T(8,128)(2,1)} async-done(((bf16[3,1536,1536]{2,1,0:T(8,128)(2,1)}), bf16[3,192,1536]{2,1,0:T(8,128)(2,1)}) %reduce-scatter.29.cloned.1.call-update) | async-done | bytes 1769488 | tf_op jit(solution)/shard_map/reduce_scatter | solution.py:258
  1196.5 158.3 %reduce-scatter.27.cloned.1.call-done = bf16[8,192,384]{2,1,0:T(8,128)(2,1)} async-done(((bf16[8,1536,384]{2,1,0:T(8,128)(2,1)}), bf16[8,192,384]{2,1,0:T(8,128)(2,1)}) %reduce-scatter.27.cloned.1.call-update) | async-done | bytes 1179664 | tf_op jit(solution)/shard_map/reduce_scatter | solution.py:255
  1358.6 40.9 %all-reduce = (f32[8]{0:T(128)S(1)}, f32[3]{0:T(128)S(1)}) all-reduce(f32[8]{0:T(128)S(1)} %get-tuple-element.180, f32[3]{0:T(128)S(1)} %get-tuple-element.177), channel_id=1, replica_groups=mesh['dp'=8,'tensor'=4] {'dp','tensor'}, use_global_device_ids=true, to_apply=%region_33.34 | all-reduce | flops 11 | bytes 88 | tf_op jit(solution)/shard_map/psum | solution.py:267
  1404.8 130.6 %all-gather.30.cloned.1.call-done = bf16[8,1536,384]{2,1,0:T(8,128)(2,1)} async-done(((bf16[8,192,384]{2,1,0:T(8,128)(2,1)}), bf16[8,1536,384]{2,1,0:T(8,128)(2,1)}) %all-gather.30.cloned.1.call-update) | async-done | bytes 9437200 | tf_op jit(solution)/shard_map/all_gather | solution.py:279
  1549.5 182.0 %all-gather.34.cloned.1.call-done = bf16[3,1536,1536]{2,1,0:T(8,128)(2,1)} async-done(((bf16[3,192,1536]{2,1,0:T(8,128)(2,1)}), bf16[3,1536,1536]{2,1,0:T(8,128)(2,1)}) %all-gather.34.cloned.1.call-update) | async-done | bytes 14155792 | tf_op jit(solution)/shard_map/all_gather | solution.py:282
  1731.5 19.1 convolution_convert_fusion.11
  1750.9 123.7 %all-reduce.16.cloned.1.call-done = (bf16[8,1536,192]{1,2,0:T(8,128)(2,1)}, bf16[3,1536,192]{1,2,0:T(8,128)(2,1)}) async-done(((bf16[8,1536,192]{1,2,0:T(8,128)(2,1)}, bf16[3,1536,192]{1,2,0:T(8,128)(2,1)}), (bf16[8,1536,192]{1,2,0:T(8,128)(2,1)}, bf16[3,1536,192]{1,2,0:T(8,128)(2,1)})) %all-reduce.16.cloned.1.call-update) | async-done | bytes 6488080 | tf_op jit(solution)/shard_map/psum | solution.py:302
  1902.2 16.5 convolution_convert_fusion.10
  1919.2 122.7 %all-reduce.14.cloned.1.call-done = (bf16[8,1536,192]{1,2,0:T(8,128)(2,1)}, bf16[3,1536,192]{1,2,0:T(8,128)(2,1)}) async-done(((bf16[8,1536,192]{1,2,0:T(8,128)(2,1)}, bf16[3,1536,192]{1,2,0:T(8,128)(2,1)}), (bf16[8,1536,192]{1,2,0:T(8,128)(2,1)}, bf16[3,1536,192]{1,2,0:T(8,128)(2,1)})) %all-reduce.14.cloned.1.call-update) | async-done | bytes 6488080 | tf_op jit(solution)/shard_map/psum | solution.py:326
  2078.7 108.2 %all-gather.32.cloned.1.call-done = bf16[8,1536,384]{2,1,0:T(8,128)(2,1)} async-done(((bf16[8,192,384]{2,1,0:T(8,128)(2,1)}), bf16[8,1536,384]{2,1,0:T(8,128)(2,1)}) %all-gather.32.cloned.1.call-update) | async-done | bytes 9437200 | tf_op jit(solution)/shard_map/all_gather | solution.py:279
  2201.0 182.2 %all-gather.36.cloned.1.call-done = bf16[3,1536,1536]{2,1,0:T(8,128)(2,1)} async-done(((bf16[3,192,1536]{2,1,0:T(8,128)(2,1)}), bf16[3,1536,1536]{2,1,0:T(8,128)(2,1)}) %all-gather.36.cloned.1.call-update) | async-done | bytes 14155792 | tf_op jit(solution)/shard_map/all_gather | solution.py:282
  2383.2 19.0 convolution_convert_fusion.9
  2409.3 16.0 reduce-scatter.25.cloned.1.call-done
  2430.3 120.9 %all-reduce.12.cloned.1.call-done = (bf16[8,1536,192]{1,2,0:T(8,128)(2,1)}, bf16[3,1536,192]{1,2,0:T(8,128)(2,1)}) async-done(((bf16[8,1536,192]{1,2,0:T(8,128)(2,1)}, bf16[3,1536,192]{1,2,0:T(8,128)(2,1)}), (bf16[8,1536,192]{1,2,0:T(8,128)(2,1)}, bf16[3,1536,192]{1,2,0:T(8,128)(2,1)})) %all-reduce.12.cloned.1.call-update) | async-done | bytes 6488080 | tf_op jit(solution)/shard_map/psum | solution.py:308
  2570.6 16.5 convolution_convert_fusion.8
  2587.1 14.9 convolution_convert_fusion.4
  2608.2 32.5 %reduce-scatter.33.cloned.1.call-done = bf16[192,3]{1,0:T(8,128)(2,1)} async-done(((bf16[1536,3]{1,0:T(8,128)(2,1)}), bf16[192,3]{1,0:T(8,128)(2,1)}) %reduce-scatter.33.cloned.1.call-update) | async-done | bytes 1168
  2648.7 118.2 %all-reduce.10.cloned.1.call-done = (bf16[8,1536,192]{1,2,0:T(8,128)(2,1)}, bf16[3,1536,192]{1,2,0:T(8,128)(2,1)}) async-done(((bf16[8,1536,192]{1,2,0:T(8,128)(2,1)}, bf16[3,1536,192]{1,2,0:T(8,128)(2,1)}), (bf16[8,1536,192]{1,2,0:T(8,128)(2,1)}, bf16[3,1536,192]{1,2,0:T(8,128)(2,1)})) %all-reduce.10.cloned.1.call-update) | async-done | bytes 6488080 | tf_op jit(solution)/shard_map/psum | solution.py:326
  (347 shorter events, 469.1 us)
Async XLA Ops:
  7.2 324.2 %copy-start = (bf16[1,130,1536]{2,1,0:T(8,128)(2,1)S(1)}, bf16[1,130,1536]{2,1,0:T(8,128)(2,1)}, u32[]{:S(2)}) copy-start(bf16[1,130,1536]{2,1,0:T(8,128)(2,1)} %param.11) | copy-start | bytes 1198084
  7.2 61.6 %all-gather.14.cloned.1.call-start = ((), (), s32[]{:S(2)}) async-start(), calls=%async_computation.10 | async-start | bytes 4055040 | tf_op jit(solution)/shard_map/all_gather | solution.py:112
  38.6 166.8 %all-gather.16.cloned.1.call-start = ((), (), s32[]{:S(2)}) async-start(), calls=%async_computation.11 | async-start | bytes 10616832 | tf_op jit(solution)/shard_map/all_gather | solution.py:140
  39.3 288.7 %reduce-scatter.15.cloned.1.call-start = ((), (), s32[]{:S(2)}) async-start(), calls=%async_computation.12 | async-start | bytes 8110080 | tf_op jit(solution)/shard_map/reduce_scatter | solution.py:115
  41.0 180.4 %copy-start.30 = (f32[1056,16]{0,1:T(8,128)}, f32[1056,16]{0,1:T(8,128)S(1)}, u32[]{:S(2)}) copy-start(f32[1056,16]{0,1:T(8,128)S(1)} %get-tuple-element.211) | copy-start | bytes 202756
  266.7 93.9 %all-gather.18.cloned.1.call-start = ((), (), s32[]{:S(2)}) async-start(), calls=%async_computation.13 | async-start | bytes 4055040 | tf_op jit(solution)/shard_map/all_gather | solution.py:112
  331.3 105.1 %reduce-scatter.17.cloned.1.call-start = ((), (), s32[]{:S(2)}) async-start(), calls=%async_computation.14 | async-start | bytes 8110080 | tf_op jit(solution)/shard_map/reduce_scatter | solution.py:115
  376.1 254.8 %all-gather.22.cloned.1.call-start = ((), (), s32[]{:S(2)}) async-start(), calls=%async_computation.16 | async-start | bytes 15925248 | tf_op jit(solution)/shard_map/all_gather | solution.py:141
  376.7 286.5 %all-gather.20.cloned.1.call-start = ((), (), s32[]{:S(2)}) async-start(), calls=%async_computation.15 | async-start | bytes 4055040 | tf_op jit(solution)/shard_map/all_gather | solution.py:112
  440.6 253.3 %all-gather.24.cloned.1.call-start = ((), (), s32[]{:S(2)}) async-start(), calls=%async_computation.18 | async-start | bytes 4055040 | tf_op jit(solution)/shard_map/all_gather | solution.py:118
  441.4 323.0 %reduce-scatter.21.cloned.1.call-start = ((), (), s32[]{:S(2)}) async-start(), calls=%async_computation.19 | async-start | bytes 4055040 | tf_op jit(solution)/shard_map/reduce_scatter | solution.py:121
  725.7 101.3 %reduce-scatter.19.cloned.1.call-start = ((), (), s32[]{:S(2)}) async-start(), calls=%async_computation.17 | async-start | bytes 8110080 | tf_op jit(solution)/shard_map/reduce_scatter | solution.py:115
  735.6 126.5 %all-gather.26.cloned.1.call-start = ((), (), s32[]{:S(2)}) async-start(), calls=%async_computation.20 | async-start | bytes 4055040 | tf_op jit(solution)/shard_map/all_gather | solution.py:118
  832.9 90.4 %reduce-scatter.23.cloned.1.call-start = ((), (), s32[]{:S(2)}) async-start(), calls=%async_computation.21 | async-start | bytes 4055040 | tf_op jit(solution)/shard_map/reduce_scatter | solution.py:207
  884.7 85.9 %all-gather.28.cloned.1.call-start = ((), (), s32[]{:S(2)}) async-start(), calls=%async_computation.22 | async-start | bytes 4055040 | tf_op jit(solution)/shard_map/all_gather | solution.py:118
  929.9 260.2 %reduce-scatter.29.cloned.1.call-start = ((), (), s32[]{:S(2)}) async-start(), calls=%async_computation.25 | async-start | bytes 15925248 | tf_op jit(solution)/shard_map/reduce_scatter | solution.py:258
  959.4 395.5 %reduce-scatter.27.cloned.1.call-start = ((), (), s32[]{:S(2)}) async-start(), calls=%async_computation.24 | async-start | bytes 10616832 | tf_op jit(solution)/shard_map/reduce_scatter | solution.py:255
  1079.2 456.2 %all-gather.30.cloned.1.call-start = ((), (), s32[]{:S(2)}) async-start(), calls=%async_computation.26 | async-start | bytes 10616832 | tf_op jit(solution)/shard_map/all_gather | solution.py:279
  1358.6 176.8 %copy-start.13 = (f32[8,192,384]{2,1,0:T(8,128)}, f32[8,192,384]{2,1,0:T(8,128)S(1)}, u32[]{:S(2)}) copy-start(f32[8,192,384]{2,1,0:T(8,128)S(1)} %get-tuple-element.181) | copy-start | bytes 7077892
  1400.9 330.6 %all-gather.34.cloned.1.call-start = ((), (), s32[]{:S(2)}) async-start(), calls=%async_computation.28 | async-start | bytes 15925248 | tf_op jit(solution)/shard_map/all_gather | solution.py:282
  1404.8 469.8 %all-reduce.16.cloned.1.call-start = ((), (), s32[]{:S(2)}) async-start(), calls=%async_computation.35 | async-start | bytes 12976128 | tf_op jit(solution)/shard_map/psum | solution.py:302
  1750.6 291.3 %all-reduce.14.cloned.1.call-start = ((), (), s32[]{:S(2)}) async-start(), calls=%async_computation.34 | async-start | bytes 12976128 | tf_op jit(solution)/shard_map/psum | solution.py:326
  1918.7 268.2 %all-gather.32.cloned.1.call-start = ((), (), s32[]{:S(2)}) async-start(), calls=%async_computation.27 | async-start | bytes 10616832 | tf_op jit(solution)/shard_map/all_gather | solution.py:279
  2052.1 134.8 %copy-start.8 = (f32[8,192,384]{2,1,0:T(8,128)}, f32[8,192,384]{2,1,0:T(8,128)S(1)}, u32[]{:S(2)}) copy-start(f32[8,192,384]{2,1,0:T(8,128)S(1)} %get-tuple-element.217) | copy-start | bytes 7077892
  2052.2 331.0 %all-gather.36.cloned.1.call-start = ((), (), s32[]{:S(2)}) async-start(), calls=%async_computation.29 | async-start | bytes 15925248 | tf_op jit(solution)/shard_map/all_gather | solution.py:282
  2066.5 358.8 %reduce-scatter.25.cloned.1.call-start = ((), (), s32[]{:S(2)}) async-start(), calls=%async_computation.23 | async-start | bytes 4055040 | tf_op jit(solution)/shard_map/reduce_scatter | solution.py:121
  2078.4 472.8 %all-reduce.12.cloned.1.call-start = ((), (), s32[]{:S(2)}) async-start(), calls=%async_computation.33 | async-start | bytes 12976128 | tf_op jit(solution)/shard_map/psum | solution.py:308
  2402.2 199.9 %reduce-scatter.31.cloned.1.call-start = ((), (), s32[]{:S(2)}) async-start(), calls=%async_computation.30 | async-start | bytes 983040
  2409.2 231.4 %reduce-scatter.33.cloned.1.call-start = ((), (), s32[]{:S(2)}) async-start(), calls=%async_computation.31 | async-start | bytes 442368
  2430.1 336.8 %all-reduce.10.cloned.1.call-start = ((), (), s32[]{:S(2)}) async-start(), calls=%async_computation.32 | async-start | bytes 12976128 | tf_op jit(solution)/shard_map/psum | solution.py:326
  2604.6 173.1 %slice-start.4 = ((s8[14155776]{0:T(1024)(128)(4,1)}), s8[1572864]{0:T(1024)(128)(4,1)S(1)}, s32[]{:S(2)}) async-start(s8[14155776]{0:T(1024)(128)(4,1)} %bitcast.352), calls=%async_computation.40 | async-start | bytes 3145728
  2648.1 129.6 %copy-start.54 = (f32[3,192]{1,0:T(4,128)}, f32[3,192]{1,0:T(4,128)S(1)}, u32[]{:S(2)}) copy-start(f32[3,192]{1,0:T(4,128)S(1)} %get-tuple-element.176) | copy-start | bytes 6916
  (73 other events, 860.7 us)
Sparse Core Ops, SparseCore 0:
  38.7 30.0 all-gather.13
  70.9 134.3 all-gather.15
  266.8 61.2 reduce-scatter.14
  331.4 29.0 all-gather.17
  376.2 60.1 reduce-scatter.16
  438.5 192.4 all-gather.21
  633.1 30.1 all-gather.19
  664.8 29.0 all-gather.23
  725.8 38.4 reduce-scatter.20
  766.8 60.1 reduce-scatter.18
  833.1 29.0 all-gather.25
  884.8 38.4 reduce-scatter.22
  930.0 29.0 all-gather.27
  962.6 227.4 reduce-scatter.28
  1193.5 161.2 reduce-scatter.26
  1401.0 134.3 all-gather.29
  1538.0 193.4 all-gather.33
  1750.7 123.8 all-reduce.15
  1918.8 122.9 all-reduce.13
  2052.3 134.5 all-gather.31
  2189.7 193.4 all-gather.35
  2385.7 39.5 reduce-scatter.24
  2428.4 122.7 all-reduce.11
  2553.6 23.3 reduce-scatter.30
  2580.3 60.3 reduce-scatter.32
  2643.1 123.7 all-reduce.9
where the time goes:
time: 2800 us; the launch traced here: 2790 us
  waiting for transfers between devices  2110 us (75%)
  matrix products  494 us (18%)
  other arithmetic  71.9 us (3%)
  blocking collectives  71.6 us (3%)
  local copies, waits for them, and re-layouts  29.1 us (1%)
    all_gather x2, waiting for transfers between devices, shards(): lax.all_gather(local_mlp.astype(jnp.bfloat16), 'dp', axis=1, tiled=True)  364 us
    psum x2, waiting for transfers between devices, shards(): lax.psum(part_attn.astype(jnp.bfloat16), 'tensor').astype(jnp.float32)  245 us
    psum x2, waiting for transfers between devices, shards(): lax.psum(jnp.einsum('mdr,mcr->mdc', whole_attn, single_attn, precision=hi...  241 us
    all_gather x2, waiting for transfers between devices, shards(): lax.all_gather(local_attn.astype(jnp.bfloat16), 'dp', axis=1, tiled=True)  239 us
    all_gather x1, waiting for transfers between devices, shards(): lax.all_gather(mlp_weights, 'dp', axis=1, tiled=True)  190 us
    reduce_scatter x3, waiting for transfers between devices, collect_rows(): lax.psum_scatter(value_rows, 'tensor', scatter_dimension=1, tiled=True)  181 us
    reduce_scatter x1, waiting for transfers between devices, shards(): lax.psum_scatter(attn_terms.astype(jnp.bfloat16), 'dp', scatter_dimension...  158 us
    all_gather x1, waiting for transfers between devices, shards(): lax.all_gather(attn_weights, 'dp', axis=1, tiled=True)  137 us
  transfers between devices with their start and end apart: 26, of which 24 were waited for; matrix products, arithmetic and copies ran while one was open for 12% of the time, Pallas kernels for 0%

commit v1 on v0

v1 whole, which is shorter than its diff:
```python
import functools
import math

import jax
import jax.numpy as jnp
from jax import lax
from jax.experimental import pallas as pl
from jax.experimental.pallas import tpu as pltpu
from jax.sharding import PartitionSpec as P

D = 1536
HD = 64
FF = 6144
NS_ITERS = 2


ns_linear = 3.4445
ns_cubic = -4.775
ns_quintic = 2.0315
muon_rate = 0.2
gain_rate = 0.001
norm_epsilon = 1e-05
muon_epsilon = 1e-07


MESH_ID = pl.DeviceIdType.MESH
CHUNKS = 4
ANY = pl.BlockSpec(memory_space=pl.ANY)
VM = pl.BlockSpec(memory_space=pltpu.VMEM)


def greet(peers):
    barrier = pltpu.get_barrier_semaphore()
    for peer in peers:
        pl.semaphore_signal(barrier, inc=1, device_id=peer, device_id_type=MESH_ID)
    pl.semaphore_wait(barrier, len(peers))


def flip(value, bit):
    if bit == 1:
        return value + 1 - 2 * lax.rem(value, 2)
    return lax.rem(value + 2, 4)


def gather_body(chunks, x_ref, o_ref, send_sem, recv_sem, local_sem):
    d = lax.axis_index("dp")
    t = lax.axis_index("tensor")
    core, chip = flip(t, 1), flip(t, 2)
    width = x_ref.shape[1] // chunks
    greet([(d, core), (d, chip)])
    local = pltpu.make_async_copy(x_ref, o_ref.at[t], local_sem)
    local.start()
    firsts = []
    for j in range(chunks):
        cols = pl.ds(j * width, width)
        firsts.append(
            pltpu.make_async_remote_copy(
                x_ref.at[:, cols], o_ref.at[t, :, cols],
                send_sem.at[j], recv_sem.at[j], device_id=(d, chip), device_id_type=MESH_ID,
            )
        )
        firsts[-1].start()
    side = pltpu.make_async_remote_copy(
        x_ref, o_ref.at[t], send_sem.at[2 * chunks], recv_sem.at[2 * chunks],
        device_id=(d, core), device_id_type=MESH_ID,
    )
    side.start()
    passes = []
    for j in range(chunks):
        cols = pl.ds(j * width, width)
        firsts[j].wait_recv()
        passes.append(
            pltpu.make_async_remote_copy(
                o_ref.at[chip, :, cols], o_ref.at[chip, :, cols],
                send_sem.at[chunks + j], recv_sem.at[chunks + j],
                device_id=(d, core), device_id_type=MESH_ID,
            )
        )
        passes[-1].start()
    for j in range(chunks):
        firsts[j].wait_send()
        passes[j].wait()
    side.wait()
    local.wait()


def tensor_gather(x, cid, chunks=CHUNKS):
    rows, cols = x.shape
    return pl.pallas_call(
        functools.partial(gather_body, chunks),
        out_shape=jax.ShapeDtypeStruct((4, rows, cols), x.dtype),
        in_specs=[VM], out_specs=ANY,
        scratch_shapes=[pltpu.SemaphoreType.DMA((2 * chunks + 1,)),
                        pltpu.SemaphoreType.DMA((2 * chunks + 1,)),
                        pltpu.SemaphoreType.DMA],
        compiler_params=pltpu.CompilerParams(collective_id=cid, has_side_effects=True),
        name=f"tensor_gather_{cid}",
    )(x)


def scatter_body(chunks, p_ref, o_ref, far, own, chipsum, other, far_s, far_r, own_s, own_r, oth_s, oth_r):
    d = lax.axis_index("dp")
    t = lax.axis_index("tensor")
    core, chip = flip(t, 1), flip(t, 2)
    diag = flip(core, 2)
    width = p_ref.shape[2] // chunks
    greet([(d, core), (d, chip)])
    fars, owns, others = [], [], []
    for j in range(chunks):
        cols = pl.ds(j * width, width)
        fars.append(pltpu.make_async_remote_copy(
            p_ref.at[diag, :, cols], far.at[j], far_s.at[j], far_r.at[j],
            device_id=(d, core), device_id_type=MESH_ID))
        fars[-1].start()
    for j in range(chunks):
        cols = pl.ds(j * width, width)
        owns.append(pltpu.make_async_remote_copy(
            p_ref.at[core, :, cols], own.at[j], own_s.at[j], own_r.at[j],
            device_id=(d, core), device_id_type=MESH_ID))
        owns[-1].start()
    for j in range(chunks):
        cols = pl.ds(j * width, width)
        fars[j].wait_recv()
        chipsum[j] = (p_ref[chip, :, cols].astype(jnp.float32) + far[j].astype(jnp.float32)).astype(chipsum.dtype)
        others.append(pltpu.make_async_remote_copy(
            chipsum.at[j], other.at[j], oth_s.at[j], oth_r.at[j],
            device_id=(d, chip), device_id_type=MESH_ID))
        others[-1].start()
    for j in range(chunks):
        cols = pl.ds(j * width, width)
        owns[j].wait_recv()
        others[j].wait_recv()
        o_ref[:, cols] = (p_ref[t, :, cols].astype(jnp.float32) + own[j].astype(jnp.float32)
                          + other[j].astype(jnp.float32)).astype(o_ref.dtype)
    for j in range(chunks):
        fars[j].wait_send()
        owns[j].wait_send()
        others[j].wait_send()


def tensor_scatter(p, cid, out_dtype=jnp.float32, chunks=CHUNKS):
    _, rows, cols = p.shape
    width = cols // chunks
    dma = pltpu.SemaphoreType.DMA((chunks,))
    buf = pltpu.VMEM((chunks, rows, width), p.dtype)
    return pl.pallas_call(
        functools.partial(scatter_body, chunks),
        out_shape=jax.ShapeDtypeStruct((rows, cols), out_dtype),
        in_specs=[VM], out_specs=VM,
        scratch_shapes=[buf, buf, buf, buf, dma, dma, dma, dma, dma, dma],
        compiler_params=pltpu.CompilerParams(collective_id=cid, has_side_effects=True),
        name=f"tensor_scatter_{cid}",
    )(p)


def swap_body(count, x_ref, o_ref, bounce, send_sem, recv_sem, local_sem):
    d = lax.axis_index("dp")
    t = lax.axis_index("tensor")
    greet([(lax.rem(d + k, count), t) for k in range(1, count)])
    copies = []
    for k in range(1, count):
        peer = lax.rem(d + k, count)
        copies.append(pltpu.make_async_remote_copy(
            x_ref.at[peer], o_ref.at[d], send_sem.at[k], recv_sem.at[k],
            device_id=(peer, t), device_id_type=MESH_ID))
        copies[-1].start()
    inward = pltpu.make_async_copy(x_ref.at[d], bounce, local_sem.at[0])
    inward.start()
    inward.wait()
    outward = pltpu.make_async_copy(bounce, o_ref.at[d], local_sem.at[1])
    outward.start()
    for copy in copies:
        copy.wait()
    outward.wait()


def dp_swap(x, cid):
    count, rows, cols = x.shape
    return pl.pallas_call(
        functools.partial(swap_body, count),
        out_shape=jax.ShapeDtypeStruct(x.shape, x.dtype),
        in_specs=[ANY], out_specs=ANY,
        scratch_shapes=[pltpu.VMEM((rows, cols), x.dtype),
                        pltpu.SemaphoreType.DMA((count,)), pltpu.SemaphoreType.DMA((count,)),
                        pltpu.SemaphoreType.DMA((2,))],
        compiler_params=pltpu.CompilerParams(collective_id=cid, has_side_effects=True),
        name=f"dp_swap_{cid}",
    )(x)


ROOTS = (2, 5, 3)


def root_gather_body(count, roots, x_ref, o_ref, bounce, send_sem, recv_sem, local_sem):
    d = lax.axis_index("dp")
    t = lax.axis_index("tensor")
    greet([(lax.rem(d + k, count), t) for k in range(1, count)])
    for step in range(len(roots)):
        for e in range(count):
            m = (e + step) % len(roots)
            root = roots[m]
            if e == root:
                continue
            copy = pltpu.make_async_remote_copy(
                x_ref.at[m], o_ref.at[e], send_sem.at[m], recv_sem.at[e],
                device_id=(root, t), device_id_type=MESH_ID)

            @pl.when(d == e)
            def _():
                copy.start()

    for m, root in enumerate(roots):
        @pl.when(d == root)
        def _():
            inward = pltpu.make_async_copy(x_ref.at[m], bounce, local_sem.at[0])
            inward.start()
            inward.wait()
            outward = pltpu.make_async_copy(bounce, o_ref.at[root], local_sem.at[1])
            outward.start()
            outward.wait()
            for e in range(count):
                if e != root:
                    pltpu.make_async_remote_copy(
                        x_ref.at[m], o_ref.at[e], send_sem.at[m], recv_sem.at[e],
                        device_id=(root, t), device_id_type=MESH_ID).wait_recv()

        @pl.when(d != root)
        def _():
            pltpu.make_async_remote_copy(
                x_ref.at[m], o_ref.at[0], send_sem.at[m], recv_sem.at[0],
                device_id=(root, t), device_id_type=MESH_ID).wait_send()


def root_gather(x, count, cid, roots=ROOTS):
    _, rows, cols = x.shape
    return pl.pallas_call(
        functools.partial(root_gather_body, count, roots),
        out_shape=jax.ShapeDtypeStruct((count, rows, cols), x.dtype),
        in_specs=[ANY], out_specs=ANY,
        scratch_shapes=[pltpu.VMEM((rows, cols), x.dtype),
                        pltpu.SemaphoreType.DMA((len(roots),)), pltpu.SemaphoreType.DMA((count,)),
                        pltpu.SemaphoreType.DMA((2,))],
        compiler_params=pltpu.CompilerParams(collective_id=cid, has_side_effects=True),
        name=f"root_gather_{cid}",
    )(x)


def root_spread_body(count, roots, x_ref, o_ref, bounce, send_sem, recv_sem, local_sem):
    d = lax.axis_index("dp")
    t = lax.axis_index("tensor")
    greet([(lax.rem(d + k, count), t) for k in range(1, count)])
    for m, root in enumerate(roots):
        @pl.when(d == root)
        def _():
            copies = []
            for e in range(count):
                if e != root:
                    copies.append(pltpu.make_async_remote_copy(
                        x_ref.at[e], o_ref.at[m], send_sem.at[e], recv_sem.at[m],
                        device_id=(e, t), device_id_type=MESH_ID))
                    copies[-1].start()
            inward = pltpu.make_async_copy(x_ref.at[root], bounce, local_sem.at[0])
            inward.start()
            inward.wait()
            outward = pltpu.make_async_copy(bounce, o_ref.at[m], local_sem.at[1])
            outward.start()
            outward.wait()
            for copy in copies:
                copy.wait_send()

        @pl.when(d != root)
        def _():
            pltpu.make_async_remote_copy(
                x_ref.at[0], o_ref.at[m], send_sem.at[0], recv_sem.at[m],
                device_id=(root, t), device_id_type=MESH_ID).wait_recv()


def root_spread(x, matrices, cid, roots=ROOTS):
    count, rows, cols = x.shape
    return pl.pallas_call(
        functools.partial(root_spread_body, count, roots),
        out_shape=jax.ShapeDtypeStruct((matrices, rows, cols), x.dtype),
        in_specs=[ANY], out_specs=ANY,
        scratch_shapes=[pltpu.VMEM((rows, cols), x.dtype),
                        pltpu.SemaphoreType.DMA((count,)), pltpu.SemaphoreType.DMA((matrices,)),
                        pltpu.SemaphoreType.DMA((2,))],
        compiler_params=pltpu.CompilerParams(collective_id=cid, has_side_effects=True),
        name=f"root_spread_{cid}",
    )(x)


def layer_norm(value_rows, gain):
    center = value_rows - jnp.mean(value_rows, axis=-1, keepdims=True)
    spread = jnp.mean(center * center, axis=-1, keepdims=True)
    return center * lax.rsqrt(spread + norm_epsilon) * gain


def rotate(value_rows, direction):
    pair_count = HD // 4
    inverse = jnp.exp(jnp.arange(pair_count, dtype=jnp.float32) * (-math.log(10000.0) / pair_count))
    positions = jnp.arange(value_rows.shape[1], dtype=jnp.float32)
    angles = positions[:, None] * inverse[None, :]
    cosine = jnp.cos(angles)[None, :, None, :]
    sine_part = direction * jnp.sin(angles)[None, :, None, :]
    leading = value_rows[..., :pair_count]
    trailing = value_rows[..., pair_count : 2 * pair_count]
    untouched = value_rows[..., 2 * pair_count :]
    return jnp.concatenate(
        [
            leading * cosine - trailing * sine_part,
            trailing * cosine + leading * sine_part,
            untouched,
        ],
        axis=-1,
    )


def attend_forward(query, keys, value, length):
    scores = jnp.einsum("ihd,jhd->hij", query, keys, preferred_element_type=jnp.float32)
    usable = jnp.arange(keys.shape[0], dtype=jnp.int32) < length
    scaled = jnp.where(usable[None, None, :], scores * 0.125, -1000000000.0)
    biggest = jnp.max(scaled, axis=-1, keepdims=True)
    logsum = biggest + jnp.log(jnp.sum(jnp.exp(scaled - biggest), axis=-1, keepdims=True))
    weights = jnp.exp(scaled - logsum).astype(jnp.bfloat16)
    output = jnp.einsum("hij,jhd->ihd", weights, value, preferred_element_type=jnp.float32)
    return (output.astype(jnp.bfloat16), logsum)


def attend_backward(query, keys, value, grad_output, logsum, length):
    scores = jnp.einsum("ihd,jhd->hij", query, keys, preferred_element_type=jnp.float32)
    usable = jnp.arange(keys.shape[0], dtype=jnp.int32) < length
    scaled = jnp.where(usable[None, None, :], scores * 0.125, -1000000000.0)
    probs = jnp.exp(scaled - logsum)
    grad_probs = jnp.einsum("ihd,jhd->hij", grad_output, value, preferred_element_type=jnp.float32)
    grad_value = jnp.einsum(
        "hij,ihd->jhd", probs.astype(jnp.bfloat16), grad_output, preferred_element_type=jnp.float32
    )
    totals = jnp.sum(probs * grad_probs, axis=-1, keepdims=True)
    grad_scores = (probs * (grad_probs - totals) * 0.125).astype(jnp.bfloat16)
    grad_query = jnp.einsum("hij,jhd->ihd", grad_scores, keys, preferred_element_type=jnp.float32)
    grad_keys = jnp.einsum("hij,ihd->jhd", grad_scores, query, preferred_element_type=jnp.float32)
    return (grad_query, grad_keys, grad_value)


def project(value_rows, weight_matrix):
    return jnp.einsum("acz,zy->acy", value_rows, weight_matrix, preferred_element_type=jnp.float32)


def expand(value_rows, weight_matrix):
    return jnp.einsum("xby,ay->xba", value_rows, weight_matrix, preferred_element_type=jnp.float32)


def outer(gradient_tree, value_rows):
    return jnp.einsum("mgf,mgx->xf", gradient_tree, value_rows, preferred_element_type=jnp.float32)

def times(left, right):
    return jnp.dot(left, right, preferred_element_type=jnp.float32)


def half(values):
    return values.astype(jnp.bfloat16)


def inner_product(values):
    return lax.dot_general(values, values, (((1,), (1,)), ((), ())), preferred_element_type=jnp.float32)


def unit_gram(gram):
    size = gram.shape[0]
    rows = lax.broadcasted_iota(jnp.int32, (size, size), 0)
    cols = lax.broadcasted_iota(jnp.int32, (size, size), 1)
    total = jnp.sum(jnp.where(rows == cols, gram.astype(jnp.float32), 0.0))
    scale = 1.0 / (jnp.sqrt(total) + muon_epsilon)
    return half(gram.astype(jnp.float32) * scale * scale), scale


def step_columns(gram, block):
    def poly(values):
        once = times(gram, half(values))
        twice = times(gram, half(once))
        return ns_linear * values + ns_cubic * once + ns_quintic * twice

    first = poly(block.astype(jnp.float32))
    single = poly(poly(times(gram, half(first))))
    double = poly(poly(times(gram, half(single))))
    return ns_linear * first + ns_cubic * single + ns_quintic * double


def step_matrix(gram, block):
    cubic_one = ns_cubic * gram.astype(jnp.float32) + ns_quintic * times(gram, gram)
    low_one = half(cubic_one)
    side = ns_linear * gram.astype(jnp.float32) + times(low_one, gram)
    low_side = half(side)
    gram_two = ns_linear * side + times(low_one, low_side)
    low_two = half(gram_two)
    cubic_two = ns_cubic * gram_two + ns_quintic * times(low_two, low_two)
    rest = ns_linear * (cubic_one + cubic_two) + times(half(cubic_two), low_one)
    return ns_linear * ns_linear * block.astype(jnp.float32) + times(half(rest), block)


def orthogonal_attn(moment):
    count, rows, cols = moment.shape
    block = dp_swap(half(moment), 4).reshape(count * rows, cols)
    whole = tensor_gather(block, 3, 3)
    gram = sum(inner_product(whole[k]) for k in range(4))
    gram, scale = unit_gram(gram)
    result = step_columns(gram, block) * (scale * -muon_rate)
    return dp_swap(half(result).reshape(count, rows, cols), 4).astype(jnp.float32)


def orthogonal_mlp(moment, count):
    matrices, rows, cols = moment.shape
    size = count * rows
    block = root_gather(half(moment), count, 7).reshape(size, cols)
    part = half(inner_product(block))
    gram = tensor_scatter(part.reshape(4, size // 4, size), 5)
    gram = tensor_gather(half(gram), 6).reshape(size, size)
    gram, scale = unit_gram(gram)
    result = step_matrix(gram, block) * (scale * (-muon_rate * max(1.0, FF / D) ** 0.5))
    return root_spread(half(result).reshape(count, rows, cols), matrices, 8).astype(jnp.float32)


def orthogonal_rows(moment, rate):
    total = lax.psum(jnp.sum(moment * moment, axis=(1, 2)), ("dp", "tensor"))
    local = moment / (jnp.sqrt(total) + muon_epsilon)[:, None, None]

    def against(gram, whole):
        return jnp.einsum("mdc,mdr->mcr", gram, whole, preferred_element_type=jnp.float32)

    for iteration in range(NS_ITERS):
        whole = lax.all_gather(half(local), "dp", axis=1, tiled=True)

        def gram_of(values):
            part = jnp.einsum("mdr,mcr->mdc", whole, half(values), preferred_element_type=jnp.float32)
            return half(lax.psum(half(part), "tensor"))

        single = against(gram_of(local), whole)
        double = against(gram_of(single), whole)
        local = ns_linear * local + ns_cubic * single + ns_quintic * double
    return -rate * local


def shards(
    latents,
    context,
    lengths,
    cotangent,
    attn_weights,
    mlp_weights,
    norm_gains,
    attn_momenta,
    mlp_momenta,
    gain_momenta,
):
    seq_count = latents.shape[0]
    inner = attn_weights.shape[2]
    head_local = inner // HD
    dp_count = lax.axis_size("dp")

    def split_heads(value_rows):
        return value_rows.reshape(value_rows.shape[0], value_rows.shape[1], head_local, HD)

    def merge_heads(value_rows):
        return value_rows.reshape(value_rows.shape[0], value_rows.shape[1], inner)

    def spread_rows(value_rows):
        _, rows, cols = value_rows.shape
        return tensor_gather(value_rows[0], 1).reshape(1, 4 * rows, cols)

    def collect_rows(value_rows):
        _, rows, cols = value_rows.shape
        return tensor_scatter(half(value_rows).reshape(4, rows // 4, cols), 2)[None]

    def forward_map(query, keys, value, length_list):
        output, logsum = attend_forward(query[0], keys[0], value[0], length_list[0])
        return output[None], logsum[None]

    def backward_map(query, keys, value, grad_output, logsum, length_list):
        grads = attend_backward(query[0], keys[0], value[0], grad_output[0], logsum[0], length_list[0])
        return tuple(grad[None] for grad in grads)

    def gather_weights(values):
        return lax.all_gather(values, "dp", axis=1, tiled=True)

    def reduce_grads(values):
        return lax.psum_scatter(
            half(jnp.stack(values)), "dp", scatter_dimension=1, tiled=True
        ).astype(jnp.float32)

    gain_values = gather_weights(norm_gains).astype(jnp.float32)
    first_full = gather_weights(attn_weights[:3])
    second_full = gather_weights(attn_weights[3:])
    mlp_full = gather_weights(mlp_weights)
    attn_full = [first_full[k] for k in range(3)] + [second_full[k] for k in range(5)]
    gradient_mixture = spread_rows(cotangent)
    resid_zero = latents.astype(jnp.float32)
    rows_one = spread_rows(half(layer_norm(resid_zero, gain_values[0])))
    query_self = half(rotate(split_heads(project(rows_one, attn_full[0])), 1.0))
    keys_self = half(rotate(split_heads(project(rows_one, attn_full[1])), 1.0))
    value_self = split_heads(half(project(rows_one, attn_full[2])))
    attended, logsum_self = forward_map(query_self, keys_self, value_self, lengths)
    attended = merge_heads(attended)
    resid_one = resid_zero + collect_rows(expand(attended, attn_full[3]))
    rows_two = spread_rows(half(layer_norm(resid_one, gain_values[1])))
    query_cross = split_heads(half(project(rows_two, attn_full[4])))
    keys_cross = split_heads(half(project(context, attn_full[5])))
    value_cross = split_heads(half(project(context, attn_full[6])))
    cond_lengths = jnp.full((seq_count,), keys_cross.shape[1], jnp.int32)
    crossed, logsum_cross = forward_map(query_cross, keys_cross, value_cross, cond_lengths)
    crossed = merge_heads(crossed)
    resid_two = resid_one + collect_rows(expand(crossed, attn_full[7]))
    rows_three = spread_rows(half(layer_norm(resid_two, gain_values[2])))
    gate = project(rows_three, mlp_full[0])
    upward = project(rows_three, mlp_full[1])
    hidden_state = half(jax.nn.silu(gate) * upward)
    grad_hidden = jnp.einsum(
        "zpc,cx->zpx", gradient_mixture, mlp_full[2], preferred_element_type=jnp.float32
    )
    unused_value, gate_pull = jax.vjp(
        lambda gate_in, up_in: jax.nn.silu(gate_in) * up_in, gate, upward
    )
    grad_gate, grad_up = gate_pull(grad_hidden)
    grad_gate = half(grad_gate)
    grad_up = half(grad_up)
    down_weight = jnp.einsum(
        "moj,mor->rj", hidden_state, gradient_mixture, preferred_element_type=jnp.float32
    )
    weight_gate = outer(grad_gate, rows_three)
    weight_up = outer(grad_up, rows_three)
    mlp_grad = reduce_grads([weight_gate, weight_up, down_weight])
    normed_three_grad = collect_rows(
        expand(grad_gate, mlp_full[0]) + expand(grad_up, mlp_full[1])
    )
    unused_norm, norm_pull = jax.vjp(layer_norm, resid_two, gain_values[2])
    resid_grad, gain_three = norm_pull(normed_three_grad)
    grad_two = cotangent.astype(jnp.float32) + resid_grad
    grad_cross_out = spread_rows(half(grad_two))
    result = half(resid_two + collect_rows(expand(hidden_state, mlp_full[2])))
    weight_cross_out = outer(crossed, grad_cross_out)
    grad_crossed = split_heads(half(project(grad_cross_out, attn_full[7])))
    grad_q_cross, grad_k_cross, grad_v_cross = backward_map(
        query_cross, keys_cross, value_cross, grad_crossed, logsum_cross, cond_lengths
    )
    grad_q_cross = merge_heads(half(grad_q_cross))
    grad_k_cross = merge_heads(half(grad_k_cross))
    grad_v_cross = merge_heads(half(grad_v_cross))
    weight_q_cross = outer(grad_q_cross, rows_two)
    weight_k_cross = outer(grad_k_cross, context)
    weight_v_cross = outer(grad_v_cross, context)
    cond_partial = expand(grad_k_cross, attn_full[5]) + expand(grad_v_cross, attn_full[6])
    context_grad = lax.psum_scatter(
        half(cond_partial), "tensor", scatter_dimension=2, tiled=True
    ).astype(jnp.float32)
    normed_two_grad = collect_rows(expand(grad_q_cross, attn_full[4]))
    unused_norm, norm_pull = jax.vjp(layer_norm, resid_one, gain_values[1])
    resid_grad, gain_two = norm_pull(normed_two_grad)
    grad_one = grad_two + resid_grad
    grad_self_out = spread_rows(half(grad_one))
    weight_self_out = outer(attended, grad_self_out)
    late_grad = reduce_grads(
        [weight_self_out, weight_q_cross, weight_k_cross, weight_v_cross, weight_cross_out]
    )
    grad_attended = split_heads(half(project(grad_self_out, attn_full[3])))
    grad_q_self, grad_k_self, grad_v_self = backward_map(
        query_self, keys_self, value_self, grad_attended, logsum_self, lengths
    )
    grad_q_self = merge_heads(half(rotate(grad_q_self, -1.0)))
    grad_k_self = merge_heads(half(rotate(grad_k_self, -1.0)))
    grad_v_self = merge_heads(half(grad_v_self))
    early_grad = reduce_grads(
        [outer(grad_q_self, rows_one), outer(grad_k_self, rows_one), outer(grad_v_self, rows_one)]
    )
    normed_one_grad = collect_rows(
        expand(grad_q_self, attn_full[0])
        + expand(grad_k_self, attn_full[1])
        + expand(grad_v_self, attn_full[2])
    )
    unused_norm, norm_pull = jax.vjp(layer_norm, resid_zero, gain_values[0])
    resid_grad, gain_one = norm_pull(normed_one_grad)
    latent_grad = grad_one + resid_grad
    gain_whole = lax.psum(jnp.stack([gain_one, gain_two, gain_three]), ("dp", "tensor"))
    gain_width = norm_gains.shape[1]
    gain_grad = lax.dynamic_slice_in_dim(gain_whole, lax.axis_index("dp") * gain_width, gain_width, 1)
    attn_grad = jnp.concatenate([early_grad, late_grad])
    attn_moment = 0.5 * attn_momenta + 0.5 * attn_grad
    mlp_moment = 0.5 * mlp_momenta + 0.5 * mlp_grad
    if dp_count == attn_weights.shape[0] and NS_ITERS == 2:
        mlp_step = orthogonal_mlp(mlp_moment, dp_count)
        attn_step = orthogonal_attn(attn_moment)
    else:
        mlp_step = orthogonal_rows(mlp_moment, muon_rate * max(1.0, FF / D) ** 0.5)
        attn_step = orthogonal_rows(attn_moment, muon_rate)
    gain_moment = 0.5 * gain_momenta + 0.5 * gain_grad
    gain_step = -gain_rate * gain_moment
    return (
        result,
        latent_grad,
        context_grad,
        attn_grad,
        mlp_grad,
        gain_grad,
        attn_moment,
        mlp_moment,
        gain_moment,
        attn_step,
        mlp_step,
        gain_step,
    )


def solution(mesh):
    in_specs = (
        P("dp", "tensor", None),
        P("dp", None, None),
        P("dp"),
        P("dp", "tensor", None),
        P(None, "dp", "tensor"),
        P(None, "dp", "tensor"),
        P(None, "dp"),
        P(None, "dp", "tensor"),
        P(None, "dp", "tensor"),
        P(None, "dp"),
    )
    out_specs = (
        P("dp", "tensor", None),
        P("dp", "tensor", None),
        P("dp", None, "tensor"),
        P(None, "dp", "tensor"),
        P(None, "dp", "tensor"),
        P(None, "dp"),
        P(None, "dp", "tensor"),
        P(None, "dp", "tensor"),
        P(None, "dp"),
        P(None, "dp", "tensor"),
        P(None, "dp", "tensor"),
        P(None, "dp"),
    )
    return jax.shard_map(shards, mesh=mesh, in_specs=in_specs, out_specs=out_specs, check_vma=False)
```

time: 2800 us -> 1580 us (0.56)
  waiting for transfers between devices: 2110 us -> 254 us
  Pallas kernels: 0 us -> 674 us
  matrix products: 494 us -> 433 us
    all_gather x12 -> x3, waiting for transfers between devices: 1050 us -> 90.9 us  [gather_weights(): return lax.all_gather(values, 'dp', axis=1, tiled=True)]
    pallas_call x0 -> x19, Pallas kernels: none -> 674 us  [the longest x8 200 us: tensor_gather(): pl.pallas_call(functools.partial(gather_body, chunks), out_shape=jax.Shap...]
    psum x4 -> x0, waiting for transfers between devices: 486 us -> none  [the longest x2 245 us: shards(): lax.psum(part_attn.astype(jnp.bfloat16), 'tensor').astype(jnp.float32)]
    reduce_scatter x8 -> x3, waiting for transfers between devices: 533 us -> 163 us  [reduce_grads(): lax.psum_scatter(half(jnp.stack(values)), 'dp', scatter_dimension=1, tile...]
    dot_general x17 -> x23, matrix products: 217 us -> 161 us  [the longest x17 120 us: times(): return jnp.dot(left, right, preferred_element_type=jnp.float32)]
    unnamed x28 -> x8, waiting for transfers between devices: 34.8 us -> 0.78 us
  transfers between devices with their start and end apart: 26 -> 7, of which waited for: 24 -> 4; matrix products, arithmetic and copies ran while one was open for 12% -> 15% of each run, Pallas kernels for 0% -> 18%
where the time goes in v1:
time: 1580 us; the launch traced here: 1570 us
  Pallas kernels  674 us (43%)
  matrix products  433 us (27%)
  waiting for transfers between devices  254 us (16%)
  other arithmetic  93.6 us (6%)
  blocking collectives  67.7 us (4%)
  local copies, waits for them, and re-layouts  32.3 us (2%)
  between operations  17.9 us (1%)
    pallas_call x8, Pallas kernels, tensor_gather(): pl.pallas_call(functools.partial(gather_body, chunks), out_shape=jax.Shap...  200 us
    pallas_call x7, Pallas kernels, tensor_scatter(): pl.pallas_call(functools.partial(scatter_body, chunks), out_shape=jax.Sha...  185 us
    reduce_scatter x3, waiting for transfers between devices, reduce_grads(): lax.psum_scatter(half(jnp.stack(values)), 'dp', scatter_dimension=1, tile...  163 us
    pallas_call x1, Pallas kernels, root_spread(): pl.pallas_call(functools.partial(root_spread_body, count, roots), out_sha...  150 us
    dot_general x17, matrix products, times(): return jnp.dot(left, right, preferred_element_type=jnp.float32)  120 us
    all_gather x3, waiting for transfers between devices, gather_weights(): return lax.all_gather(values, 'dp', axis=1, tiled=True)  90.9 us
    pallas_call x2, Pallas kernels, dp_swap(): pl.pallas_call(functools.partial(swap_body, count), out_shape=jax.ShapeDt...  89.6 us
    dot_general x11, matrix products, expand(): jnp.einsum('xby,ay->xba', value_rows, weight_matrix, preferred_element_ty...  56.1 us
  transfers between devices with their start and end apart: 7, of which 4 were waited for; matrix products, arithmetic and copies ran while one was open for 15% of the time, Pallas kernels for 18%

profile of v1, /device:TPU:26, one launch (start us, length us, event | category | flops | bytes accessed | tf_op | source)
XLA Modules:
  0.0 1574.3 jit_solution(4920006043109323668)
XLA Ops:
  12.1 25.1 %all-gather = bf16[8,192,3]{1,2,0:T(4,128)(2,1)S(1)} all-gather(bf16[1,192,3]{1,2,0:T(4,128)(2,1)S(1)} %bitcast.399), channel_id=1, replica_groups=mesh['dp'=8,'tensor'=4] {'dp'}, dimensions={0}, use_global_device_ids=true | all-gather | bytes 10368 | tf_op jit(solution)/shard_map/all_gather | solution.py:483
  39.3 23.1 %tensor_gather_1.6 = bf16[4,264,1536]{2,1,0:T(8,128)(2,1)} custom-call(bf16[264,1536]{1,0:T(8,128)(2,1)} %fusion.161.x_ref), custom_call_target="tpu_custom_call" | custom-call | tf_op jit(solution)/shard_map/tensor_gather_1/pallas_call | solution.py:89
  63.0 23.3 %tensor_gather_1.9 = bf16[4,264,1536]{2,1,0:T(8,128)(2,1)} custom-call(bf16[264,1536]{1,0:T(8,128)(2,1)} %bitcast.332), custom_call_target="tpu_custom_call" | custom-call | tf_op jit(solution)/shard_map/tensor_gather_1/pallas_call | solution.py:89
  131.7 13.7 fusion.75
  145.4 23.8 %all-gather.7.cloned.1.call-done = bf16[5,1536,384]{2,1,0:T(8,128)(2,1)} async-done(((bf16[5,192,384]{2,1,0:T(8,128)(2,1)}), bf16[5,1536,384]{2,1,0:T(8,128)(2,1)}) %all-gather.7.cloned.1.call-update) | async-done | bytes 5898256 | tf_op jit(solution)/shard_map/all_gather | solution.py:483
  174.1 25.2 %tensor_scatter_2.6 = f32[264,1536]{1,0:T(8,128)} custom-call(bf16[4,264,1536]{2,1,0:T(8,128)(2,1)} %bitcast.361), custom_call_target="tpu_custom_call" | custom-call | tf_op jit(solution)/shard_map/tensor_scatter_2/pallas_call | solution.py:146
  204.4 22.9 %tensor_gather_1.7 = bf16[4,264,1536]{2,1,0:T(8,128)(2,1)} custom-call(bf16[264,1536]{1,0:T(8,128)(2,1)} %fusion.159.x_ref), custom_call_target="tpu_custom_call" | custom-call | tf_op jit(solution)/shard_map/tensor_gather_1/pallas_call | solution.py:89
  245.5 25.1 %tensor_scatter_2.7 = f32[264,1536]{1,0:T(8,128)} custom-call(bf16[4,264,1536]{2,1,0:T(8,128)(2,1)} %bitcast.362), custom_call_target="tpu_custom_call" | custom-call | tf_op jit(solution)/shard_map/tensor_scatter_2/pallas_call | solution.py:146
  274.8 23.0 %tensor_gather_1.8 = bf16[4,264,1536]{2,1,0:T(8,128)(2,1)} custom-call(bf16[264,1536]{1,0:T(8,128)(2,1)} %fusion.160.x_ref), custom_call_target="tpu_custom_call" | custom-call | tf_op jit(solution)/shard_map/tensor_gather_1/pallas_call | solution.py:89
  297.8 67.0 %all-gather.9.cloned.1.call-done = bf16[3,1536,1536]{2,1,0:T(8,128)(2,1)} async-done(((bf16[3,192,1536]{2,1,0:T(8,128)(2,1)}), bf16[3,1536,1536]{2,1,0:T(8,128)(2,1)}) %all-gather.9.cloned.1.call-update) | async-done | bytes 14155792 | tf_op jit(solution)/shard_map/all_gather | solution.py:483
  414.1 25.2 %tensor_scatter_2.9 = f32[264,1536]{1,0:T(8,128)} custom-call(bf16[4,264,1536]{2,1,0:T(8,128)(2,1)} %bitcast.359), custom_call_target="tpu_custom_call" | custom-call | tf_op jit(solution)/shard_map/tensor_scatter_2/pallas_call | solution.py:146
  451.5 24.9 %tensor_scatter_2.8 = f32[264,1536]{1,0:T(8,128)} custom-call(bf16[4,264,1536]{2,1,0:T(8,128)(2,1)} %bitcast.360), custom_call_target="tpu_custom_call" | custom-call | tf_op jit(solution)/shard_map/tensor_scatter_2/pallas_call | solution.py:146
  482.6 23.0 %tensor_gather_1.10 = bf16[4,264,1536]{2,1,0:T(8,128)(2,1)} custom-call(bf16[264,1536]{1,0:T(8,128)(2,1)} %fusion.158.x_ref), custom_call_target="tpu_custom_call" | custom-call | tf_op jit(solution)/shard_map/tensor_gather_1/pallas_call | solution.py:89
  530.4 25.1 %tensor_scatter_2.10 = f32[264,1536]{1,0:T(8,128)} custom-call(bf16[4,264,1536]{2,1,0:T(8,128)(2,1)} %bitcast.363), custom_call_target="tpu_custom_call" | custom-call | tf_op jit(solution)/shard_map/tensor_scatter_2/pallas_call | solution.py:146
  560.6 22.9 %tensor_gather_1.11 = bf16[4,264,1536]{2,1,0:T(8,128)(2,1)} custom-call(bf16[264,1536]{1,0:T(8,128)(2,1)} %convert_bitcast_fusion.x_ref), custom_call_target="tpu_custom_call" | custom-call | tf_op jit(solution)/shard_map/tensor_gather_1/pallas_call | solution.py:89
  589.2 29.7 %fusion.55 = f32[1,1056,6,64]{1,3,2,0:T(8,128)} fusion(f32[6,1056,1056]{1,2,0:T(8,128)} %get-tuple-element.107, f32[6,1056]{1,0:T(8,128)S(1)} %log_add_fusion.1, bf16[1056,6,64]{0,2,1:T(8,128)(2,1)S(1)} %bitcast.356, bf16[1056,6,64]{0,2,1:T(8,128)(2,1)S(1)} %bitcast.352, bf16[1056,6,32]{0,2,1:T(8,128)(2,1)S(1)} %copy-done.47, ...), kind=kOutput, calls=%fused_computation.93 | convolution fusion | flops 2618549504 | bytes 30843648 | tf_op jit(solution)/shard_map/hij,jhd->ihd/dot_general | solution.py:340
  619.0 30.3 %fusion.60 = f32[1,1056,6,64]{1,3,2,0:T(8,128)} fusion(f32[6,1056,1056]{1,2,0:T(8,128)} %get-tuple-element.107, f32[6,1056]{1,0:T(8,128)S(1)} %log_add_fusion.1, bf16[1056,6,64]{0,2,1:T(8,128)(2,1)S(1)} %bitcast.357, bf16[1056,6,64]{0,2,1:T(8,128)(2,1)S(1)} %bitcast.353, bf16[1056,6,32]{0,2,1:T(8,128)(2,1)S(1)} %copy-done.45, ...), kind=kOutput, calls=%fused_computation.94 | convolution fusion | flops 2618549504 | bytes 30843648 | tf_op jit(solution)/shard_map/hij,ihd->jhd/dot_general | solution.py:341
  749.7 25.3 %tensor_scatter_2.11 = f32[264,1536]{1,0:T(8,128)} custom-call(bf16[4,264,1536]{2,1,0:T(8,128)(2,1)} %bitcast.331), custom_call_target="tpu_custom_call" | custom-call | tf_op jit(solution)/shard_map/tensor_scatter_2/pallas_call | solution.py:146
  779.4 42.6 %psum.7 = f32[3,1536]{1,0:T(4,128)S(1)} all-reduce(f32[3,1536]{1,0:T(4,128)S(1)} %pad_maximum_fusion.10), channel_id=1, replica_groups=mesh['dp'=8,'tensor'=4] {'dp','tensor'}, use_global_device_ids=true, to_apply=%region_25.26 | all-reduce | flops 4608 | bytes 36864 | tf_op jit(solution)/shard_map/psum | solution.py:581
  830.1 76.0 %reduce-scatter.9.cloned.1.call-done = bf16[5,192,384]{2,1,0:T(8,128)(2,1)} async-done(((bf16[5,1536,384]{2,1,0:T(8,128)(2,1)}), bf16[5,192,384]{2,1,0:T(8,128)(2,1)}) %reduce-scatter.9.cloned.1.call-update) | async-done | bytes 737296 | tf_op jit(solution)/shard_map/reduce_scatter | solution.py:486
  911.1 57.5 %dp_swap_4.2 = bf16[8,192,384]{2,1,0:T(8,128)(2,1)} custom-call(bf16[8,192,384]{2,1,0:T(8,128)(2,1)} %get-tuple-element.74.x_ref), custom_call_target="tpu_custom_call" | custom-call | tf_op jit(solution)/shard_map/dp_swap_4/pallas_call | solution.py:179
  968.6 31.2 %tensor_gather_3.1 = bf16[4,1536,384]{2,1,0:T(8,128)(2,1)} custom-call(bf16[1536,384]{1,0:T(8,128)(2,1)} %bitcast.346), custom_call_target="tpu_custom_call" | custom-call | tf_op jit(solution)/shard_map/tensor_gather_3/pallas_call | solution.py:89
  1056.7 32.1 %dp_swap_4.3 = bf16[8,192,384]{2,1,0:T(8,128)(2,1)} custom-call(bf16[8,192,384]{2,1,0:T(8,128)(2,1)} %bitcast.387), custom_call_target="tpu_custom_call" | custom-call | tf_op jit(solution)/shard_map/dp_swap_4/pallas_call | solution.py:179
  1091.7 86.8 %reduce-scatter.11.cloned.1.call-done = bf16[3,192,1536]{2,1,0:T(8,128)(2,1)} async-done(((bf16[3,1536,1536]{2,1,0:T(8,128)(2,1)}), bf16[3,192,1536]{2,1,0:T(8,128)(2,1)}) %reduce-scatter.11.cloned.1.call-update) | async-done | bytes 1769488 | tf_op jit(solution)/shard_map/reduce_scatter | solution.py:486
  1185.7 48.8 %root_gather_7.1 = bf16[8,192,1536]{2,1,0:T(8,128)(2,1)} custom-call(bf16[3,192,1536]{2,1,0:T(8,128)(2,1)} %get-tuple-element.71.x_ref), custom_call_target="tpu_custom_call" | custom-call | tf_op jit(solution)/shard_map/root_gather_7/pallas_call | solution.py:236
  1247.6 33.9 %tensor_scatter_5.1 = f32[384,1536]{1,0:T(8,128)} custom-call(bf16[4,384,1536]{2,1,0:T(8,128)(2,1)} %bitcast.345), custom_call_target="tpu_custom_call" | custom-call | tf_op jit(solution)/shard_map/tensor_scatter_5/pallas_call | solution.py:146
  1284.3 31.0 %tensor_gather_6.1 = bf16[4,384,1536]{2,1,0:T(8,128)(2,1)} custom-call(bf16[384,1536]{1,0:T(8,128)(2,1)} %convert_element_type.383.x_ref), custom_call_target="tpu_custom_call" | custom-call | tf_op jit(solution)/shard_map/tensor_gather_6/pallas_call | solution.py:89
  1328.2 13.8 fusion.13
  1351.8 15.6 multiply_add_fusion.1
  1367.4 17.7 %multiply_add_fusion = f32[1536,1536]{1,0:T(8,128)} fusion(f32[1536,1536]{1,0:T(8,128)} %multiply_add_fusion.1), kind=kOutput, calls=%fused_computation.35 | convolution fusion | flops 7257194496 | bytes 18874368 | tf_op jit(solution)/shard_map/dot_general | solution.py:357
  1385.1 27.9 %multiply_convert_fusion = bf16[1536,1536]{1,0:T(8,128)(2,1)} fusion(bf16[1536,1536]{1,0:T(8,128)(2,1)} %bitcast.341, f32[]{:T(128)S(6)} %mul.875, f32[1536,1536]{1,0:T(8,128)} %copy-done.67, f32[1536,1536]{1,0:T(8,128)} %multiply_add_fusion), kind=kOutput, calls=%fused_computation.33 | convolution fusion | flops 14521466880 | bytes 28311556 | tf_op jit(solution)/shard_map/dot_general | solution.py:357
  1413.1 150.4 %root_spread_8.1 = bf16[3,192,1536]{2,1,0:T(8,128)(2,1)} custom-call(bf16[8,192,1536]{2,1,0:T(8,128)(2,1)} %bitcast.344), custom_call_target="tpu_custom_call" | custom-call | tf_op jit(solution)/shard_map/root_spread_8/pallas_call | solution.py:280
  (301 shorter events, 412.3 us)
Async XLA Ops:
  7.2 192.1 %copy-start = (bf16[1,130,1536]{2,1,0:T(8,128)(2,1)S(1)}, bf16[1,130,1536]{2,1,0:T(8,128)(2,1)}, u32[]{:S(2)}) copy-start(bf16[1,130,1536]{2,1,0:T(8,128)(2,1)} %param.11) | copy-start | bytes 1198084
  7.2 30.2 %copy-start.4 = (bf16[1,264,1536]{2,1,0:T(8,128)(2,1)S(1)}, bf16[1,264,1536]{2,1,0:T(8,128)(2,1)}, u32[]{:S(2)}) copy-start(bf16[1,264,1536]{2,1,0:T(8,128)(2,1)} %param.10) | copy-start | bytes 2433028
  7.2 80.1 %all-gather.5.cloned.1.call-start = ((), (), s32[]{:S(2)}) async-start(), calls=%async_computation.4 | async-start | bytes 3981312 | tf_op jit(solution)/shard_map/all_gather | solution.py:483
  9.2 160.0 %all-gather.7.cloned.1.call-start = ((), (), s32[]{:S(2)}) async-start(), calls=%async_computation.5 | async-start | bytes 6635520 | tf_op jit(solution)/shard_map/all_gather | solution.py:483
  11.3 353.5 %all-gather.9.cloned.1.call-start = ((), (), s32[]{:S(2)}) async-start(), calls=%async_computation.6 | async-start | bytes 15925248 | tf_op jit(solution)/shard_map/all_gather | solution.py:483
  12.1 815.4 %reduce-scatter.13.cloned.1.call-start = ((), (), s32[]{:S(2)}) async-start(), calls=%async_computation.10 | async-start | bytes 983040
  37.6 24.7 %copy-start.56 = (f32[264]{0:T(512)}, f32[264]{0:T(512)S(1)}, u32[]{:S(2)}) copy-start(f32[264]{0:T(512)S(1)} %broadcast_multiply_fusion.5) | copy-start | bytes 3172
  38.0 48.3 %copy-start.61 = (f32[264]{0:T(512)}, f32[264]{0:T(512)S(1)}, u32[]{:S(2)}) copy-start(f32[264]{0:T(512)S(1)} %fusion.115) | copy-start | bytes 3172
  38.0 48.3 %copy-start.58 = (f32[264]{0:T(512)}, f32[264]{0:T(512)S(1)}, u32[]{:S(2)}) copy-start(f32[264]{0:T(512)S(1)} %fusion.176) | copy-start | bytes 3172
  87.3 18.8 %copy-start.42 = (f32[1056,16]{0,1:T(8,128)}, f32[1056,16]{0,1:T(8,128)S(1)}, u32[]{:S(2)}) copy-start(f32[1056,16]{0,1:T(8,128)S(1)} %get-tuple-element.105) | copy-start | bytes 202756
  106.4 12.3 copy-start.49
  106.4 12.3 copy-start.51
  106.4 12.3 copy-start.52
  106.4 12.3 copy-start.53
  118.7 13.0 copy-start.17
  145.4 28.7 %copy-start.37 = (bf16[6,64,1056]{2,1,0:T(8,128)(2,1)}, bf16[6,64,1056]{2,1,0:T(8,128)(2,1)S(1)}, u32[]{:S(2)}) copy-start(bf16[6,64,1056]{2,1,0:T(8,128)(2,1)S(1)} %fusion.75) | copy-start | bytes 2433028
  589.2 29.8 %copy-start.21 = (bf16[1056,384]{0,1:T(8,128)(2,1)}, bf16[1056,384]{0,1:T(8,128)(2,1)S(1)}, u32[]{:S(2)}) copy-start(bf16[1056,384]{0,1:T(8,128)(2,1)S(1)} %copy.93) | copy-start | bytes 2433028
  589.2 29.8 %copy-start.45 = (bf16[1056,6,32]{0,2,1:T(8,128)(2,1)S(1)}, bf16[1056,6,32]{0,2,1:T(8,128)(2,1)}, u32[]{:S(2)}) copy-start(bf16[1056,6,32]{0,2,1:T(8,128)(2,1)} %copy-done.44) | copy-start | bytes 1216516
  589.2 29.8 %copy-start.50 = (bf16[1056,6,16]{0,2,1:T(8,128)(2,1)S(1)}, bf16[1056,6,16]{0,2,1:T(8,128)(2,1)}, u32[]{:S(2)}) copy-start(bf16[1056,6,16]{0,2,1:T(8,128)(2,1)} %copy-done.49) | copy-start | bytes 608260
  684.2 145.9 %reduce-scatter.7.cloned.1.call-start = ((), (), s32[]{:S(2)}) async-start(), calls=%async_computation.7 | async-start | bytes 3981312 | tf_op jit(solution)/shard_map/reduce_scatter | solution.py:486
  695.3 210.8 %reduce-scatter.9.cloned.1.call-start = ((), (), s32[]{:S(2)}) async-start(), calls=%async_computation.8 | async-start | bytes 6635520 | tf_op jit(solution)/shard_map/reduce_scatter | solution.py:486
  711.1 467.3 %reduce-scatter.11.cloned.1.call-start = ((), (), s32[]{:S(2)}) async-start(), calls=%async_computation.9 | async-start | bytes 15925248 | tf_op jit(solution)/shard_map/reduce_scatter | solution.py:486
  749.6 25.4 %copy-start.60 = (f32[1536]{0:T(1024)S(1)}, f32[1536]{0:T(1024)}, u32[]{:S(2)}) copy-start(f32[1536]{0:T(1024)} %get-tuple-element.62) | copy-start | bytes 18436
  749.6 25.4 %copy-start.5 = (bf16[1,264,1536]{2,1,0:T(8,128)(2,1)S(1)}, bf16[1,264,1536]{2,1,0:T(8,128)(2,1)}, u32[]{:S(2)}) copy-start(bf16[1,264,1536]{2,1,0:T(8,128)(2,1)} %param.10) | copy-start | bytes 2433028
  749.6 25.4 %copy-start.55 = (f32[1536]{0:T(1024)S(1)}, f32[1536]{0:T(1024)}, u32[]{:S(2)}) copy-start(f32[1536]{0:T(1024)} %copy-done.54) | copy-start | bytes 18436
  749.6 25.4 %copy-start.57 = (f32[264]{0:T(512)S(1)}, f32[264]{0:T(512)}, u32[]{:S(2)}) copy-start(f32[264]{0:T(512)} %copy-done.56) | copy-start | bytes 3172
  749.6 27.4 %copy-start.62 = (f32[264]{0:T(512)S(1)}, f32[264]{0:T(512)}, u32[]{:S(2)}) copy-start(f32[264]{0:T(512)} %copy-done.61) | copy-start | bytes 3172
  749.6 27.4 %copy-start.59 = (f32[264]{0:T(512)S(1)}, f32[264]{0:T(512)}, u32[]{:S(2)}) copy-start(f32[264]{0:T(512)} %copy-done.58) | copy-start | bytes 3172
  775.0 47.0 %copy-start.63 = (f32[3,192]{1,0:T(4,128)S(1)}, f32[3,192]{1,0:T(4,128)}, u32[]{:S(2)}) copy-start(f32[3,192]{1,0:T(4,128)} %param.19) | copy-start | bytes 6916
  775.0 48.3 %copy-start.9 = (f32[1,264,1536]{2,1,0:T(8,128)S(1)}, f32[1,264,1536]{2,1,0:T(8,128)}, u32[]{:S(2)}) copy-start(f32[1,264,1536]{2,1,0:T(8,128)} %copy-done.7) | copy-start | bytes 4866052
  1328.2 13.8 copy-start.15
  1413.1 154.1 %copy-start.1 = (bf16[1,130,1536]{2,1,0:T(8,128)(2,1)S(1)}, bf16[1,130,1536]{2,1,0:T(8,128)(2,1)}, u32[]{:S(2)}) copy-start(bf16[1,130,1536]{2,1,0:T(8,128)(2,1)} %param.11) | copy-start | bytes 1198084
  (47 other events, 242.0 us)
Sparse Core Ops, SparseCore 0:
  10.8 63.5 all-gather.4
  77.1 92.0 all-gather.6
  171.4 193.3 all-gather.8
  684.3 23.7 reduce-scatter.12
  712.2 78.1 reduce-scatter.6
  793.8 112.1 reduce-scatter.8
  909.7 268.7 reduce-scatter.10

commit v2 on v1

--- a/solution.py
+++ b/solution.py
@@ -94,6 +94,7 @@
                         pltpu.SemaphoreType.DMA((2 * chunks + 1,)),
                         pltpu.SemaphoreType.DMA],
         compiler_params=pltpu.CompilerParams(collective_id=cid, has_side_effects=True),
+        cost_estimate=pl.CostEstimate(flops=0, bytes_accessed=75900000, transcendentals=0),
         name=f"tensor_gather_{cid}",
     )(x)
 
@@ -149,6 +150,7 @@
         in_specs=[VM], out_specs=VM,
         scratch_shapes=[buf, buf, buf, buf, dma, dma, dma, dma, dma, dma],
         compiler_params=pltpu.CompilerParams(collective_id=cid, has_side_effects=True),
+        cost_estimate=pl.CostEstimate(flops=0, bytes_accessed=82500000, transcendentals=0),
         name=f"tensor_scatter_{cid}",
     )(p)
 
@@ -184,108 +186,41 @@
                         pltpu.SemaphoreType.DMA((count,)), pltpu.SemaphoreType.DMA((count,)),
                         pltpu.SemaphoreType.DMA((2,))],
         compiler_params=pltpu.CompilerParams(collective_id=cid, has_side_effects=True),
+        cost_estimate=pl.CostEstimate(flops=0, bytes_accessed=125400000, transcendentals=0),
         name=f"dp_swap_{cid}",
     )(x)
 
 
-ROOTS = (2, 5, 3)
-
-
-def root_gather_body(count, roots, x_ref, o_ref, bounce, send_sem, recv_sem, local_sem):
+ROOTS = (2, 5, 0)
+
+
+def small_body(count, x_ref, o_ref, send_sem, recv_sem, local_sem):
     d = lax.axis_index("dp")
     t = lax.axis_index("tensor")
     greet([(lax.rem(d + k, count), t) for k in range(1, count)])
-    for step in range(len(roots)):
-        for e in range(count):
-            m = (e + step) % len(roots)
-            root = roots[m]
-            if e == root:
-                continue
-            copy = pltpu.make_async_remote_copy(
-                x_ref.at[m], o_ref.at[e], send_sem.at[m], recv_sem.at[e],
-                device_id=(root, t), device_id_type=MESH_ID)
-
-            @pl.when(d == e)
-            def _():
-                copy.start()
-
-    for m, root in enumerate(roots):
-        @pl.when(d == root)
-        def _():
-            inward = pltpu.make_async_copy(x_ref.at[m], bounce, local_sem.at[0])
-            inward.start()
-            inward.wait()
-            outward = pltpu.make_async_copy(bounce, o_ref.at[root], local_sem.at[1])
-            outward.start()
-            outward.wait()
-            for e in range(count):
-                if e != root:
-                    pltpu.make_async_remote_copy(
-                        x_ref.at[m], o_ref.at[e], send_sem.at[m], recv_sem.at[e],
-                        device_id=(root, t), device_id_type=MESH_ID).wait_recv()
-
-        @pl.when(d != root)
-        def _():
-            pltpu.make_async_remote_copy(
-                x_ref.at[m], o_ref.at[0], send_sem.at[m], recv_sem.at[0],
-                device_id=(root, t), device_id_type=MESH_ID).wait_send()
-
-
-def root_gather(x, count, cid, roots=ROOTS):
-    _, rows, cols = x.shape
+    copies = []
+    for k in range(1, count):
+        copies.append(pltpu.make_async_remote_copy(
+            x_ref, o_ref.at[d], send_sem.at[k], recv_sem.at[k],
+            device_id=(lax.rem(d + k, count), t), device_id_type=MESH_ID))
+        copies[-1].start()
+    local = pltpu.make_async_copy(x_ref, o_ref.at[d], local_sem)
+    local.start()
+    for copy in copies:
+        copy.wait()
+    local.wait()
+
+
+def small_gather(x, count, cid):
+    dma = pltpu.SemaphoreType.DMA((count,))
     return pl.pallas_call(
-        functools.partial(root_gather_body, count, roots),
-        out_shape=jax.ShapeDtypeStruct((count, rows, cols), x.dtype),
-        in_specs=[ANY], out_specs=ANY,
-        scratch_shapes=[pltpu.VMEM((rows, cols), x.dtype),
-                        pltpu.SemaphoreType.DMA((len(roots),)), pltpu.SemaphoreType.DMA((count,)),
-                        pltpu.SemaphoreType.DMA((2,))],
+        functools.partial(small_body, count),
+        out_shape=jax.ShapeDtypeStruct((count,) + x.shape, x.dtype),
+        in_specs=[VM], out_specs=VM,
+        scratch_shapes=[dma, dma, pltpu.SemaphoreType.DMA],
         compiler_params=pltpu.CompilerParams(collective_id=cid, has_side_effects=True),
-        name=f"root_gather_{cid}",
-    )(x)
-
-
-def root_spread_body(count, roots, x_ref, o_ref, bounce, send_sem, recv_sem, local_sem):
-    d = lax.axis_index("dp")
-    t = lax.axis_index("tensor")
-    greet([(lax.rem(d + k, count), t) for k in range(1, count)])
-    for m, root in enumerate(roots):
-        @pl.when(d == root)
-        def _():
-            copies = []
-            for e in range(count):
-                if e != root:
-                    copies.append(pltpu.make_async_remote_copy(
-                        x_ref.at[e], o_ref.at[m], send_sem.at[e], recv_sem.at[m],
-                        device_id=(e, t), device_id_type=MESH_ID))
-                    copies[-1].start()
-            inward = pltpu.make_async_copy(x_ref.at[root], bounce, local_sem.at[0])
-            inward.start()
-            inward.wait()
-            outward = pltpu.make_async_copy(bounce, o_ref.at[m], local_sem.at[1])
-            outward.start()
-            outward.wait()
-            for copy in copies:
-                copy.wait_send()
-
-        @pl.when(d != root)
-        def _():
-            pltpu.make_async_remote_copy(
-                x_ref.at[0], o_ref.at[m], send_sem.at[0], recv_sem.at[m],
-                device_id=(root, t), device_id_type=MESH_ID).wait_recv()
-
-
-def root_spread(x, matrices, cid, roots=ROOTS):
-    count, rows, cols = x.shape
-    return pl.pallas_call(
-        functools.partial(root_spread_body, count, roots),
-        out_shape=jax.ShapeDtypeStruct((matrices, rows, cols), x.dtype),
-        in_specs=[ANY], out_specs=ANY,
-        scratch_shapes=[pltpu.VMEM((rows, cols), x.dtype),
-                        pltpu.SemaphoreType.DMA((count,)), pltpu.SemaphoreType.DMA((matrices,)),
-                        pltpu.SemaphoreType.DMA((2,))],
-        compiler_params=pltpu.CompilerParams(collective_id=cid, has_side_effects=True),
-        name=f"root_spread_{cid}",
+        cost_estimate=pl.CostEstimate(flops=0, bytes_accessed=19800000, transcendentals=0),
+        name=f"small_gather_{cid}",
     )(x)
 
 
@@ -365,11 +300,15 @@
     return lax.dot_general(values, values, (((1,), (1,)), ((), ())), preferred_element_type=jnp.float32)
 
 
-def unit_gram(gram):
+def diagonal_sum(gram, width=128):
     size = gram.shape[0]
-    rows = lax.broadcasted_iota(jnp.int32, (size, size), 0)
-    cols = lax.broadcasted_iota(jnp.int32, (size, size), 1)
-    total = jnp.sum(jnp.where(rows == cols, gram.astype(jnp.float32), 0.0))
+    corners = jnp.stack([gram[k : k + width, k : k + width] for k in range(0, size, width)])
+    rows = lax.broadcasted_iota(jnp.int32, corners.shape, 1)
+    cols = lax.broadcasted_iota(jnp.int32, corners.shape, 2)
+    return jnp.sum(jnp.where(rows == cols, corners.astype(jnp.float32), 0.0))
+
+
+def unit_gram(gram, total):
     scale = 1.0 / (jnp.sqrt(total) + muon_epsilon)
     return half(gram.astype(jnp.float32) * scale * scale), scale
 
@@ -398,26 +337,56 @@
     return ns_linear * ns_linear * block.astype(jnp.float32) + times(half(rest), block)
 
 
-def orthogonal_attn(moment):
-    count, rows, cols = moment.shape
-    block = dp_swap(half(moment), 4).reshape(count * rows, cols)
-    whole = tensor_gather(block, 3, 3)
-    gram = sum(inner_product(whole[k]) for k in range(4))
-    gram, scale = unit_gram(gram)
+def orthogonal_attn(block, extra, shape):
+    size, cols = block.shape
+    padded = jnp.pad(half(extra), ((0, 16 - extra.shape[0]), (0, cols - extra.shape[1])))
+    whole = tensor_gather(jnp.concatenate([block, padded]), 3, 3)
+    summed = jnp.sum(whole[:, size : size + extra.shape[0], : extra.shape[1]].astype(jnp.float32), axis=0)
+    whole = whole[:, :size]
+    total = jnp.sum(jnp.square(whole.astype(jnp.float32)))
+    gram, scale = unit_gram(sum(inner_product(whole[k]) for k in range(4)), total)
     result = step_columns(gram, block) * (scale * -muon_rate)
-    return dp_swap(half(result).reshape(count, rows, cols), 4).astype(jnp.float32)
-
-
-def orthogonal_mlp(moment, count):
-    matrices, rows, cols = moment.shape
-    size = count * rows
-    block = root_gather(half(moment), count, 7).reshape(size, cols)
+    return dp_swap(half(result).reshape(shape), 4).astype(jnp.float32), summed
+
+
+def to_roots(values, roots, count):
+    d = lax.axis_index("dp")
+    pieces = []
+    for k in range(count):
+        serves = [((root + k) % count) for root in roots]
+        which = sum(m * (d == serves[m]).astype(jnp.int32) for m in range(len(roots)))
+        piece = lax.dynamic_index_in_dim(values, which, 0, keepdims=False)
+        if k:
+            piece = lax.ppermute(piece, "dp", [(serves[m], roots[m]) for m in range(len(roots))])
+        pieces.append(piece)
+    return jnp.concatenate(pieces)
+
+
+def from_roots(values, roots, count):
+    d = lax.axis_index("dp")
+    rows = values.shape[0] // count
+    pieces = []
+    for k in range(count):
+        piece = values[k * rows : (k + 1) * rows]
+        if k:
+            piece = lax.ppermute(piece, "dp", [(root, (root + k) % count) for root in roots])
+        pieces.append(piece)
+    stacked = jnp.stack(pieces)
+    return jnp.stack(
+        [
+            lax.dynamic_index_in_dim(stacked, lax.rem(d + count - root, count), 0, keepdims=False)
+            for root in roots
+        ]
+    )
+
+
+def orthogonal_mlp(block):
+    size = block.shape[0]
     part = half(inner_product(block))
     gram = tensor_scatter(part.reshape(4, size // 4, size), 5)
     gram = tensor_gather(half(gram), 6).reshape(size, size)
-    gram, scale = unit_gram(gram)
-    result = step_matrix(gram, block) * (scale * (-muon_rate * max(1.0, FF / D) ** 0.5))
-    return root_spread(half(result).reshape(count, rows, cols), matrices, 8).astype(jnp.float32)
+    gram, scale = unit_gram(gram, diagonal_sum(gram))
+    return half(step_matrix(gram, block) * (scale * (-muon_rate * max(1.0, FF / D) ** 0.5)))
 
 
 def orthogonal_rows(moment, rate):
@@ -483,15 +452,14 @@
         return lax.all_gather(values, "dp", axis=1, tiled=True)
 
     def reduce_grads(values):
-        return lax.psum_scatter(
-            half(jnp.stack(values)), "dp", scatter_dimension=1, tiled=True
-        ).astype(jnp.float32)
-
-    gain_values = gather_weights(norm_gains).astype(jnp.float32)
-    first_full = gather_weights(attn_weights[:3])
-    second_full = gather_weights(attn_weights[3:])
+        return lax.psum_scatter(values, "dp", scatter_dimension=1, tiled=True).astype(jnp.float32)
+
+    attn_full = gather_weights(attn_weights)
     mlp_full = gather_weights(mlp_weights)
-    attn_full = [first_full[k] for k in range(3)] + [second_full[k] for k in range(5)]
+    gain_count, gain_width = norm_gains.shape
+    padded = jnp.pad(norm_gains, ((0, 16 - gain_count), (0, -gain_width % 128)))
+    gain_values = small_gather(padded, dp_count, 9)[:, :gain_count, :gain_width].astype(jnp.float32)
+    gain_values = gain_values.transpose(1, 0, 2).reshape(gain_count, dp_count * gain_width)
     gradient_mixture = spread_rows(cotangent)
     resid_zero = latents.astype(jnp.float32)
     rows_one = spread_rows(half(layer_norm(resid_zero, gain_values[0])))
@@ -527,7 +495,10 @@
     )
     weight_gate = outer(grad_gate, rows_three)
     weight_up = outer(grad_up, rows_three)
-    mlp_grad = reduce_grads([weight_gate, weight_up, down_weight])
+    mlp_terms, grad_gate, grad_up, hidden_late = lax.optimization_barrier(
+        (half(jnp.stack([weight_gate, weight_up, down_weight])), grad_gate, grad_up, hidden_state)
+    )
+    mlp_grad = reduce_grads(mlp_terms)
     normed_three_grad = collect_rows(
         expand(grad_gate, mlp_full[0]) + expand(grad_up, mlp_full[1])
     )
@@ -535,7 +506,6 @@
     resid_grad, gain_three = norm_pull(normed_three_grad)
     grad_two = cotangent.astype(jnp.float32) + resid_grad
     grad_cross_out = spread_rows(half(grad_two))
-    result = half(resid_two + collect_rows(expand(hidden_state, mlp_full[2])))
     weight_cross_out = outer(crossed, grad_cross_out)
     grad_crossed = split_heads(half(project(grad_cross_out, attn_full[7])))
     grad_q_cross, grad_k_cross, grad_v_cross = backward_map(
@@ -548,18 +518,12 @@
     weight_k_cross = outer(grad_k_cross, context)
     weight_v_cross = outer(grad_v_cross, context)
     cond_partial = expand(grad_k_cross, attn_full[5]) + expand(grad_v_cross, attn_full[6])
-    context_grad = lax.psum_scatter(
-        half(cond_partial), "tensor", scatter_dimension=2, tiled=True
-    ).astype(jnp.float32)
     normed_two_grad = collect_rows(expand(grad_q_cross, attn_full[4]))
     unused_norm, norm_pull = jax.vjp(layer_norm, resid_one, gain_values[1])
     resid_grad, gain_two = norm_pull(normed_two_grad)
     grad_one = grad_two + resid_grad
     grad_self_out = spread_rows(half(grad_one))
     weight_self_out = outer(attended, grad_self_out)
-    late_grad = reduce_grads(
-        [weight_self_out, weight_q_cross, weight_k_cross, weight_v_cross, weight_cross_out]
-    )
     grad_attended = split_heads(half(project(grad_self_out, attn_full[3])))
     grad_q_self, grad_k_self, grad_v_self = backward_map(
         query_self, keys_self, value_self, grad_attended, logsum_self, lengths
@@ -567,9 +531,31 @@
     grad_q_self = merge_heads(half(rotate(grad_q_self, -1.0)))
     grad_k_self = merge_heads(half(rotate(grad_k_self, -1.0)))
     grad_v_self = merge_heads(half(grad_v_self))
-    early_grad = reduce_grads(
-        [outer(grad_q_self, rows_one), outer(grad_k_self, rows_one), outer(grad_v_self, rows_one)]
-    )
+    fast = dp_count == attn_weights.shape[0] and NS_ITERS == 2
+    mlp_moment = 0.5 * mlp_momenta + 0.5 * mlp_grad
+    mlp_low, grad_q_self, grad_k_self, grad_v_self = lax.optimization_barrier(
+        (half(mlp_moment), grad_q_self, grad_k_self, grad_v_self)
+    )
+    if fast:
+        mlp_block = to_roots(mlp_low, ROOTS, dp_count)
+    attn_terms = half(
+        jnp.stack(
+            [
+                outer(grad_q_self, rows_one),
+                outer(grad_k_self, rows_one),
+                outer(grad_v_self, rows_one),
+                weight_self_out,
+                weight_q_cross,
+                weight_k_cross,
+                weight_v_cross,
+                weight_cross_out,
+            ]
+        )
+    )
+    attn_terms, grad_q_self, grad_k_self, grad_v_self = lax.optimization_barrier(
+        (attn_terms, grad_q_self, grad_k_self, grad_v_self)
+    )
+    attn_grad = reduce_grads(attn_terms)
     normed_one_grad = collect_rows(
         expand(grad_q_self, attn_full[0])
         + expand(grad_k_self, attn_full[1])
@@ -578,16 +564,28 @@
     unused_norm, norm_pull = jax.vjp(layer_norm, resid_zero, gain_values[0])
     resid_grad, gain_one = norm_pull(normed_one_grad)
     latent_grad = grad_one + resid_grad
-    gain_whole = lax.psum(jnp.stack([gain_one, gain_two, gain_three]), ("dp", "tensor"))
-    gain_width = norm_gains.shape[1]
-    gain_grad = lax.dynamic_slice_in_dim(gain_whole, lax.axis_index("dp") * gain_width, gain_width, 1)
-    attn_grad = jnp.concatenate([early_grad, late_grad])
+    attn_grad, gain_terms, cond_terms = lax.optimization_barrier(
+        (attn_grad, half(jnp.stack([gain_one, gain_two, gain_three])), half(cond_partial))
+    )
+    gain_part = lax.psum_scatter(gain_terms, "dp", scatter_dimension=1, tiled=True)
+    context_grad = lax.psum_scatter(
+        cond_terms, "tensor", scatter_dimension=2, tiled=True
+    ).astype(jnp.float32)
+    gain_part, hidden_late = lax.optimization_barrier((gain_part, hidden_late))
+    gain_part = gain_part.astype(jnp.float32)
+    final_rows = lax.psum_scatter(
+        half(expand(hidden_late, mlp_full[2])), "tensor", scatter_dimension=1, tiled=True
+    )
+    result = half(resid_two + final_rows.astype(jnp.float32))
     attn_moment = 0.5 * attn_momenta + 0.5 * attn_grad
-    mlp_moment = 0.5 * mlp_momenta + 0.5 * mlp_grad
-    if dp_count == attn_weights.shape[0] and NS_ITERS == 2:
-        mlp_step = orthogonal_mlp(mlp_moment, dp_count)
-        attn_step = orthogonal_attn(attn_moment)
+    if fast:
+        mlp_rows = orthogonal_mlp(mlp_block)
+        mlp_rows, attn_low = lax.optimization_barrier((mlp_rows, half(attn_moment)))
+        mlp_step = from_roots(mlp_rows, ROOTS, dp_count).astype(jnp.float32)
+        attn_block = dp_swap(attn_low, 4).reshape(-1, inner)
+        attn_step, gain_grad = orthogonal_attn(attn_block, gain_part, attn_low.shape)
     else:
+        gain_grad = lax.psum(gain_part, "tensor")
         mlp_step = orthogonal_rows(mlp_moment, muon_rate * max(1.0, FF / D) ** 0.5)
         attn_step = orthogonal_rows(attn_moment, muon_rate)
     gain_moment = 0.5 * gain_momenta + 0.5 * gain_grad

time: 1580 us -> 1350 us (0.85)
  Pallas kernels: 674 us -> 560 us
  waiting for transfers between devices: 254 us -> 142 us
  blocking collectives: 67.7 us -> 0 us
  local copies, waits for them, and re-layouts: 32.3 us -> 71.2 us
  starting transfers between devices: 0.86 us -> 28.8 us
  other arithmetic: 93.6 us -> 76.9 us
    pallas_call x2 -> x1, Pallas kernels: 199 us -> 8.26 us  [small_gather(): pl.pallas_call(functools.partial(small_body, count), out_shape=jax.ShapeD...]
    reduce_scatter x3, waiting for transfers between devices: 163 us -> 0.03 us  [the longest x2 0.03 us: reduce_grads(): lax.psum_scatter(values, 'dp', scatter_dimension=1, tiled=True)]
    pallas_call x2, Pallas kernels: 89.6 us -> 186 us  [dp_swap(): pl.pallas_call(functools.partial(swap_body, count), out_shape=jax.ShapeDt...]
    ppermute x0 -> x14, waiting for transfers between devices: none -> 55.3 us  [the longest x7 39.8 us: to_roots(): lax.ppermute(piece, 'dp', [(serves[m], roots[m]) for m in range(len(roots...]
    psum x1 -> x0, blocking collectives: 42.6 us -> none  [shards(): lax.psum(jnp.stack([gain_one, gain_two, gain_three]), ('dp', 'tensor'))]
    unnamed x149 -> x225, local copies, waits for them, and re-layouts: 10.8 us -> 42.4 us
    ppermute x0 -> x14, starting transfers between devices: none -> 28.5 us  [the longest x7 19.5 us: to_roots(): lax.ppermute(piece, 'dp', [(serves[m], roots[m]) for m in range(len(roots...]
    all_gather x1 -> x0, blocking collectives: 25.1 us -> none  [gather_weights(): return lax.all_gather(values, 'dp', axis=1, tiled=True)]
  transfers between devices with their start and end apart: 7 -> 21, of which waited for: 4 -> 5; matrix products, arithmetic and copies ran while one was open for 15% -> 37% of each run, Pallas kernels for 18% -> 42%
where the time goes in v2:
time: 1350 us; the launch traced here: 1330 us
  Pallas kernels  560 us (41%)
  matrix products  438 us (32%)
  waiting for transfers between devices  142 us (11%)
  other arithmetic  76.9 us (6%)
  local copies, waits for them, and re-layouts  71.2 us (5%)
  starting transfers between devices  28.8 us (2%)
  between operations  18.4 us (1%)
    pallas_call x8, Pallas kernels, tensor_gather(): pl.pallas_call(functools.partial(gather_body, chunks), out_shape=jax.Shap...  205 us
    pallas_call x2, Pallas kernels, dp_swap(): pl.pallas_call(functools.partial(swap_body, count), out_shape=jax.ShapeDt...  186 us
    pallas_call x6, Pallas kernels, tensor_scatter(): pl.pallas_call(functools.partial(scatter_body, chunks), out_shape=jax.Sha...  160 us
    dot_general x17, matrix products, times(): return jnp.dot(left, right, preferred_element_type=jnp.float32)  120 us
    all_gather x2, waiting for transfers between devices, gather_weights(): return lax.all_gather(values, 'dp', axis=1, tiled=True)  85.5 us
    dot_general x11, matrix products, expand(): jnp.einsum('xby,ay->xba', value_rows, weight_matrix, preferred_element_ty...  58.8 us
    dot_general x10, matrix products, project(): jnp.einsum('acz,zy->acy', value_rows, weight_matrix, preferred_element_ty...  51.7 us
    unnamed x225, local copies, waits for them, and re-layouts  42.4 us
  transfers between devices with their start and end apart: 21, of which 5 were waited for; matrix products, arithmetic and copies ran while one was open for 37% of the time, Pallas kernels for 42%

profile of v2, /device:TPU:26, one launch (start us, length us, event | category | flops | bytes accessed | tf_op | source)
XLA Modules:
  0.0 1335.0 jit_solution(11180362986717359856)
XLA Ops:
  22.2 23.1 %tensor_gather_1.6 = bf16[4,264,1536]{2,1,0:T(8,128)(2,1)} custom-call(bf16[264,1536]{1,0:T(8,128)(2,1)} %fusion.175.x_ref), custom_call_target="tpu_custom_call" | custom-call | bytes 75900000 | tf_op jit(solution)/shard_map/tensor_gather_1/pallas_call | solution.py:89
  46.1 23.2 %tensor_gather_1.9 = bf16[4,264,1536]{2,1,0:T(8,128)(2,1)} custom-call(bf16[264,1536]{1,0:T(8,128)(2,1)} %bitcast.446), custom_call_target="tpu_custom_call" | custom-call | bytes 75900000 | tf_op jit(solution)/shard_map/tensor_gather_1/pallas_call | solution.py:89
  70.4 75.2 %all-gather.3.cloned.1.call-done = bf16[8,1536,384]{2,1,0:T(8,128)(2,1)} async-done(((bf16[8,192,384]{2,1,0:T(8,128)(2,1)}), bf16[8,1536,384]{2,1,0:T(8,128)(2,1)}) %all-gather.3.cloned.1.call-update) | async-done | bytes 9437200 | tf_op jit(solution)/shard_map/all_gather | solution.py:452
  165.7 12.2 fusion.225
  178.0 12.1 exponential_reduce_fusion
  190.1 13.7 %fusion.79 = bf16[6,64,1056]{2,1,0:T(8,128)(2,1)S(1)} fusion(bf16[1056,6,64]{0,2,1:T(8,128)(2,1)S(1)} %bitcast.465, f32[6,1056,1056]{1,2,0:T(8,128)} %get-tuple-element.148, f32[6,1056]{1,0:T(8,128)S(1)} %log_add_fusion.1), kind=kOutput, calls=%fused_computation.111 | convolution fusion | flops 870211584 | bytes 28410624 | tf_op jit(solution)/shard_map/hij,jhd->ihd/dot_general | solution.py:260
  209.1 25.2 %tensor_scatter_2.5 = f32[264,1536]{1,0:T(8,128)} custom-call(bf16[4,264,1536]{2,1,0:T(8,128)(2,1)} %bitcast.474), custom_call_target="tpu_custom_call" | custom-call | bytes 82500000 | tf_op jit(solution)/shard_map/tensor_scatter_2/pallas_call | solution.py:147
  238.3 22.9 %tensor_gather_1.7 = bf16[4,264,1536]{2,1,0:T(8,128)(2,1)} custom-call(bf16[264,1536]{1,0:T(8,128)(2,1)} %fusion.173.x_ref), custom_call_target="tpu_custom_call" | custom-call | bytes 75900000 | tf_op jit(solution)/shard_map/tensor_gather_1/pallas_call | solution.py:89
  278.9 25.2 %tensor_scatter_2.6 = f32[264,1536]{1,0:T(8,128)} custom-call(bf16[4,264,1536]{2,1,0:T(8,128)(2,1)} %bitcast.475), custom_call_target="tpu_custom_call" | custom-call | bytes 82500000 | tf_op jit(solution)/shard_map/tensor_scatter_2/pallas_call | solution.py:147
  307.9 23.1 %tensor_gather_1.8 = bf16[4,264,1536]{2,1,0:T(8,128)(2,1)} custom-call(bf16[264,1536]{1,0:T(8,128)(2,1)} %fusion.174.x_ref), custom_call_target="tpu_custom_call" | custom-call | bytes 75900000 | tf_op jit(solution)/shard_map/tensor_gather_1/pallas_call | solution.py:89
  360.8 13.6 %fusion.23 = (bf16[1056,1536]{1,0:T(8,128)(2,1)}, bf16[1056,1536]{1,0:T(8,128)(2,1)S(1)}, bf16[1056,1536]{1,0:T(8,128)(2,1)S(1)}) fusion(f32[1056,1536]{1,0:T(8,128)} %fusion.32, f32[1056,1536]{1,0:T(8,128)} %fusion.33, bf16[1056,1536]{1,0:T(8,128)(2,1)S(1)} %bitcast.492, bf16[3,1536,1536]{2,1,0:T(8,128)(2,1)} %all-gather.5.cloned.1.call-done), kind=kOutput, calls=%fused_computation.54 | convolution fusion | flops 5008785408 | bytes 30670848 | tf_op jit(solution)/shard_map/acz,zy->acy/dot_general | solution.py:281
  374.4 10.8 fusion.17
  423.2 25.2 %tensor_scatter_2.7 = f32[264,1536]{1,0:T(8,128)} custom-call(bf16[4,264,1536]{2,1,0:T(8,128)(2,1)} %bitcast.473), custom_call_target="tpu_custom_call" | custom-call | bytes 82500000 | tf_op jit(solution)/shard_map/tensor_scatter_2/pallas_call | solution.py:147
  454.0 23.1 %tensor_gather_1.10 = bf16[4,264,1536]{2,1,0:T(8,128)(2,1)} custom-call(bf16[264,1536]{1,0:T(8,128)(2,1)} %fusion.172.x_ref), custom_call_target="tpu_custom_call" | custom-call | bytes 75900000 | tf_op jit(solution)/shard_map/tensor_gather_1/pallas_call | solution.py:89
  500.0 25.3 %tensor_scatter_2.8 = f32[264,1536]{1,0:T(8,128)} custom-call(bf16[4,264,1536]{2,1,0:T(8,128)(2,1)} %bitcast.476), custom_call_target="tpu_custom_call" | custom-call | bytes 82500000 | tf_op jit(solution)/shard_map/tensor_scatter_2/pallas_call | solution.py:147
  531.2 23.0 %tensor_gather_1.11 = bf16[4,264,1536]{2,1,0:T(8,128)(2,1)} custom-call(bf16[264,1536]{1,0:T(8,128)(2,1)} %convert_bitcast_fusion.x_ref), custom_call_target="tpu_custom_call" | custom-call | bytes 75900000 | tf_op jit(solution)/shard_map/tensor_gather_1/pallas_call | solution.py:89
  559.8 31.3 %fusion.64 = f32[1,1056,6,64]{1,3,2,0:T(8,128)} fusion(f32[6,1056,1056]{1,2,0:T(8,128)} %get-tuple-element.148, f32[6,1056]{1,0:T(8,128)S(1)} %copy-done.61, bf16[1056,6,64]{0,2,1:T(8,128)(2,1)S(1)} %bitcast.470, bf16[1056,6,64]{0,2,1:T(8,128)(2,1)S(1)} %bitcast.466, bf16[1056,6,32]{0,2,1:T(8,128)(2,1)} %copy-done.59, bf16[1056,6,16]{0,2,1:T(8,128)(2,1)} %copy-done.68, ...), kind=kOutput, calls=%fused_computation.94 | convolution fusion | flops 2618549504 | bytes 30843648 | tf_op jit(solution)/shard_map/hij,ihd->jhd/dot_general | solution.py:276
  593.2 30.0 %fusion.59 = f32[1,1056,6,64]{1,3,2,0:T(8,128)} fusion(f32[6,1056,1056]{1,2,0:T(8,128)} %get-tuple-element.148, f32[6,1056]{1,0:T(8,128)S(1)} %copy-done.61, bf16[1056,6,64]{0,2,1:T(8,128)(2,1)S(1)} %bitcast.471, bf16[1056,6,64]{0,2,1:T(8,128)(2,1)S(1)} %bitcast.467, bf16[1056,6,32]{0,2,1:T(8,128)(2,1)S(1)} %copy-done.58, ...), kind=kOutput, calls=%fused_computation.93 | convolution fusion | flops 2618549504 | bytes 30843648 | tf_op jit(solution)/shard_map/hij,jhd->ihd/dot_general | solution.py:275
  642.6 11.4 fusion.82
  703.1 25.3 %tensor_scatter_2.9 = f32[264,1536]{1,0:T(8,128)} custom-call(bf16[4,264,1536]{2,1,0:T(8,128)(2,1)} %bitcast.445), custom_call_target="tpu_custom_call" | custom-call | bytes 82500000 | tf_op jit(solution)/shard_map/tensor_scatter_2/pallas_call | solution.py:147
  755.2 14.9 %collective-permute-done.4 = bf16[192,1536]{1,0:T(8,128)(2,1)S(1)} collective-permute-done((bf16[192,1536]{1,0:T(8,128)(2,1)S(1)}, bf16[192,1536]{1,0:T(8,128)(2,1)S(1)}, u32[]{:S(2)}, u32[]{:S(2)}) %collective-permute-start.4) | collective-permute-done | bytes 589856 | tf_op jit(solution)/shard_map/ppermute | solution.py:360
  770.1 24.9 %collective-permute-done.6 = bf16[192,1536]{1,0:T(8,128)(2,1)S(1)} collective-permute-done((bf16[192,1536]{1,0:T(8,128)(2,1)S(1)}, bf16[192,1536]{1,0:T(8,128)(2,1)S(1)}, u32[]{:S(2)}, u32[]{:S(2)}) %collective-permute-start.6) | collective-permute-done | bytes 589856 | tf_op jit(solution)/shard_map/ppermute | solution.py:360
  804.4 33.6 %tensor_scatter_5.1 = f32[384,1536]{1,0:T(8,128)} custom-call(bf16[4,384,1536]{2,1,0:T(8,128)(2,1)} %bitcast.456), custom_call_target="tpu_custom_call" | custom-call | bytes 82500000 | tf_op jit(solution)/shard_map/tensor_scatter_5/pallas_call | solution.py:147
  840.9 31.4 %tensor_gather_6.1 = bf16[4,384,1536]{2,1,0:T(8,128)(2,1)} custom-call(bf16[384,1536]{1,0:T(8,128)(2,1)} %convert_element_type.413.x_ref), custom_call_target="tpu_custom_call" | custom-call | bytes 75900000 | tf_op jit(solution)/shard_map/tensor_gather_6/pallas_call | solution.py:89
  898.9 10.8 fusion.13
  909.7 14.7 %multiply_add_fusion.1 = f32[1536,1536]{1,0:T(8,128)S(1)} fusion(f32[1536,1536]{1,0:T(8,128)} %fusion.13, f32[1536,1536]{1,0:T(8,128)} %copy-done.90), kind=kOutput, calls=%fused_computation.34 | convolution fusion | flops 7257194496 | bytes 28311552 | tf_op jit(solution)/shard_map/dot_general | solution.py:292
  924.4 10.7 multiply_add_fusion
  935.0 28.1 %multiply_convert_fusion = bf16[1536,1536]{1,0:T(8,128)(2,1)} fusion(bf16[1536,1536]{1,0:T(8,128)(2,1)} %copy-done.71, f32[]{:T(128)S(6)} %mul.884, f32[1536,1536]{1,0:T(8,128)} %copy-done.90, f32[1536,1536]{1,0:T(8,128)} %multiply_add_fusion), kind=kOutput, calls=%fused_computation.31 | convolution fusion | flops 14521466880 | bytes 28311556 | tf_op jit(solution)/shard_map/dot_general | solution.py:292
  979.8 155.7 %dp_swap_4.2 = bf16[8,192,384]{2,1,0:T(8,128)(2,1)} custom-call(bf16[8,192,384]{2,1,0:T(8,128)(2,1)} %get-tuple-element.47.x_ref), custom_call_target="tpu_custom_call" | custom-call | bytes 125400000 | tf_op jit(solution)/shard_map/dp_swap_4/pallas_call | solution.py:181
  1139.9 35.6 %tensor_gather_3.1 = bf16[4,1552,384]{2,1,0:T(8,128)(2,1)} custom-call(bf16[1552,384]{1,0:T(8,128)(2,1)} %fusion.129.x_ref), custom_call_target="tpu_custom_call" | custom-call | bytes 75900000 | tf_op jit(solution)/shard_map/tensor_gather_3/pallas_call | solution.py:89
  1257.1 30.5 %dp_swap_4.3 = bf16[8,192,384]{2,1,0:T(8,128)(2,1)} custom-call(bf16[8,192,384]{2,1,0:T(8,128)(2,1)} %bitcast.501), custom_call_target="tpu_custom_call" | custom-call | bytes 125400000 | tf_op jit(solution)/shard_map/dp_swap_4/pallas_call | solution.py:181
  1302.9 15.5 %collective-permute-done.13 = bf16[192,1536]{1,0:T(8,128)(2,1)S(1)} collective-permute-done((bf16[192,1536]{1,0:T(8,128)(2,1)S(1)}, bf16[192,1536]{1,0:T(8,128)(2,1)S(1)}, u32[]{:S(2)}, u32[]{:S(2)}) %collective-permute-start.13) | collective-permute-done | bytes 589856 | tf_op jit(solution)/shard_map/ppermute | solution.py:372
  (413 shorter events, 435.3 us)
Async XLA Ops:
  7.2 259.9 %copy-start = (bf16[1,130,1536]{2,1,0:T(8,128)(2,1)S(1)}, bf16[1,130,1536]{2,1,0:T(8,128)(2,1)}, u32[]{:S(2)}) copy-start(bf16[1,130,1536]{2,1,0:T(8,128)(2,1)} %param.11) | copy-start | bytes 1198084
  7.2 138.4 %all-gather.3.cloned.1.call-start = ((), (), s32[]{:S(2)}) async-start(), calls=%async_computation.5 | async-start | bytes 10616832 | tf_op jit(solution)/shard_map/all_gather | solution.py:452
  7.9 333.3 %all-gather.5.cloned.1.call-start = ((), (), s32[]{:S(2)}) async-start(), calls=%async_computation.6 | async-start | bytes 15925248 | tf_op jit(solution)/shard_map/all_gather | solution.py:452
  8.7 645.4 %reduce-scatter.10.cloned.1.call-start = ((), (), s32[]{:S(2)}) async-start(), calls=%async_computation.7 | async-start | bytes 15925248 | tf_op jit(solution)/shard_map/reduce_scatter | solution.py:455
  70.4 94.9 %copy-start.48 = (f32[1056,16]{0,1:T(8,128)}, f32[1056,16]{0,1:T(8,128)S(1)}, u32[]{:S(2)}) copy-start(f32[1056,16]{0,1:T(8,128)S(1)} %get-tuple-element.146) | copy-start | bytes 202756
  272.5 214.1 %copy-start.62 = (f32[6,1056]{1,0:T(8,128)}, f32[6,1056]{1,0:T(8,128)S(1)}, u32[]{:S(2)}) copy-start(f32[6,1056]{1,0:T(8,128)S(1)} %log_add_fusion) | copy-start | bytes 76036
  306.4 144.8 %copy-start.3 = (f32[1,264,1536]{2,1,0:T(8,128)}, f32[1,264,1536]{2,1,0:T(8,128)S(1)}, u32[]{:S(2)}) copy-start(f32[1,264,1536]{2,1,0:T(8,128)S(1)} %get-tuple-element.105) | copy-start | bytes 4866052
  405.1 558.1 %reduce-scatter.12.cloned.1.call-start = ((), (), s32[]{:S(2)}) async-start(), calls=%async_computation.8 | async-start | bytes 10616832 | tf_op jit(solution)/shard_map/reduce_scatter | solution.py:455
  559.8 33.4 %copy-start.28 = (bf16[1056,384]{0,1:T(8,128)(2,1)}, bf16[1056,384]{0,1:T(8,128)(2,1)S(1)}, u32[]{:S(2)}) copy-start(bf16[1056,384]{0,1:T(8,128)(2,1)S(1)} %copy.73) | copy-start | bytes 2433028
  559.8 33.4 %copy-start.58 = (bf16[1056,6,32]{0,2,1:T(8,128)(2,1)S(1)}, bf16[1056,6,32]{0,2,1:T(8,128)(2,1)}, u32[]{:S(2)}) copy-start(bf16[1056,6,32]{0,2,1:T(8,128)(2,1)} %copy-done.57) | copy-start | bytes 1216516
  593.2 33.2 %copy-start.27 = (bf16[1056,384]{0,1:T(8,128)(2,1)S(1)}, bf16[1056,384]{0,1:T(8,128)(2,1)}, u32[]{:S(2)}) copy-start(bf16[1056,384]{0,1:T(8,128)(2,1)} %copy-done.26) | copy-start | bytes 2433028
  663.7 80.1 %collective-permute-start = (bf16[192,1536]{1,0:T(8,128)(2,1)}, bf16[192,1536]{1,0:T(8,128)(2,1)}, u32[]{:S(2)}, u32[]{:S(2)}) collective-permute-start(bf16[192,1536]{1,0:T(8,128)(2,1)} %get-tuple-element.137), channel_id=1, source_target_pairs={{12,8},{24,20},{4,0},{13,9},{25,21},{5,1},{14,10},{26,22},{6,2},{1... | collective-permute-start | bytes 1769480 | tf_op jit(solution)/shard_map/ppermute | solution.py:360
  665.3 80.3 %collective-permute-start.1 = (bf16[192,1536]{1,0:T(8,128)(2,1)}, bf16[192,1536]{1,0:T(8,128)(2,1)}, u32[]{:S(2)}, u32[]{:S(2)}) collective-permute-start(bf16[192,1536]{1,0:T(8,128)(2,1)} %get-tuple-element.136), channel_id=1, source_target_pairs={{16,8},{28,20},{8,0},{17,9},{29,21},{9,1},{18,10},{30,22},{10,2},{... | collective-permute-start | bytes 1769480 | tf_op jit(solution)/shard_map/ppermute | solution.py:360
  731.3 406.5 %reduce-scatter.16.cloned.1.call-start = ((), (), s32[]{:S(2)}) async-start(), calls=%async_computation.10 | async-start | bytes 442368
  738.1 16.9 %collective-permute-start.2 = (bf16[192,1536]{1,0:T(8,128)(2,1)S(1)}, bf16[192,1536]{1,0:T(8,128)(2,1)S(1)}, u32[]{:S(2)}, u32[]{:S(2)}) collective-permute-start(bf16[192,1536]{1,0:T(8,128)(2,1)S(1)} %copy-done.56), channel_id=1, source_target_pairs={{20,8},{0,20},{12,0},{21,9},{1,21},{13,1},{22,10},{2,22},{14,2},{2... | collective-permute-start | bytes 1769480 | tf_op jit(solution)/shard_map/ppermute | solution.py:360
  738.9 16.3 %collective-permute-start.3 = (bf16[192,1536]{1,0:T(8,128)(2,1)S(1)}, bf16[192,1536]{1,0:T(8,128)(2,1)S(1)}, u32[]{:S(2)}, u32[]{:S(2)}) collective-permute-start(bf16[192,1536]{1,0:T(8,128)(2,1)S(1)} %copy-done.55), channel_id=1, source_target_pairs={{24,8},{4,20},{16,0},{25,9},{5,21},{17,1},{26,10},{6,22},{18,2},{2... | collective-permute-start | bytes 1769480 | tf_op jit(solution)/shard_map/ppermute | solution.py:360
  739.6 30.5 %collective-permute-start.4 = (bf16[192,1536]{1,0:T(8,128)(2,1)S(1)}, bf16[192,1536]{1,0:T(8,128)(2,1)S(1)}, u32[]{:S(2)}, u32[]{:S(2)}) collective-permute-start(bf16[192,1536]{1,0:T(8,128)(2,1)S(1)} %copy-done.54), channel_id=1, source_target_pairs={{28,8},{8,20},{20,0},{29,9},{9,21},{21,1},{30,10},{10,22},{22,2},{... | collective-permute-start | bytes 1769480 | tf_op jit(solution)/shard_map/ppermute | solution.py:360
  743.8 26.3 %collective-permute-start.5 = (bf16[192,1536]{1,0:T(8,128)(2,1)S(1)}, bf16[192,1536]{1,0:T(8,128)(2,1)S(1)}, u32[]{:S(2)}, u32[]{:S(2)}) collective-permute-start(bf16[192,1536]{1,0:T(8,128)(2,1)S(1)} %copy-done.53), channel_id=1, source_target_pairs={{0,8},{12,20},{24,0},{1,9},{13,21},{25,1},{2,10},{14,22},{26,2},{3... | collective-permute-start | bytes 1769480 | tf_op jit(solution)/shard_map/ppermute | solution.py:360
  745.7 49.4 %collective-permute-start.6 = (bf16[192,1536]{1,0:T(8,128)(2,1)S(1)}, bf16[192,1536]{1,0:T(8,128)(2,1)S(1)}, u32[]{:S(2)}, u32[]{:S(2)}) collective-permute-start(bf16[192,1536]{1,0:T(8,128)(2,1)S(1)} %copy-done.52), channel_id=1, source_target_pairs={{4,8},{16,20},{28,0},{5,9},{17,21},{29,1},{6,10},{18,22},{30,2},{7... | collective-permute-start | bytes 1769480 | tf_op jit(solution)/shard_map/ppermute | solution.py:360
  969.7 165.8 %copy-start.39 = (bf16[1,130,1536]{2,1,0:T(8,128)(2,1)S(1)}, bf16[1,130,1536]{2,1,0:T(8,128)(2,1)}, u32[]{:S(2)}) copy-start(bf16[1,130,1536]{2,1,0:T(8,128)(2,1)} %fusion.112) | copy-start | bytes 1198084
  970.7 352.2 %reduce-scatter.18.cloned.1.call-start = ((), (), s32[]{:S(2)}) async-start(), calls=%async_computation.11 | async-start | bytes 983040
  972.7 317.7 %collective-permute-start.7 = (bf16[192,1536]{1,0:T(8,128)(2,1)}, bf16[192,1536]{1,0:T(8,128)(2,1)}, u32[]{:S(2)}, u32[]{:S(2)}) collective-permute-start(bf16[192,1536]{1,0:T(8,128)(2,1)} %get-tuple-element.122), channel_id=1, source_target_pairs={{8,12},{20,24},{0,4},{9,13},{21,25},{1,5},{10,14},{22,26},{2,6},{1... | collective-permute-start | bytes 1769480 | tf_op jit(solution)/shard_map/ppermute | solution.py:372
  974.2 318.8 %collective-permute-start.8 = (bf16[192,1536]{1,0:T(8,128)(2,1)}, bf16[192,1536]{1,0:T(8,128)(2,1)}, u32[]{:S(2)}, u32[]{:S(2)}) collective-permute-start(bf16[192,1536]{1,0:T(8,128)(2,1)} %get-tuple-element.121), channel_id=1, source_target_pairs={{8,16},{20,28},{0,8},{9,17},{21,29},{1,9},{10,18},{22,30},{2,10},{... | collective-permute-start | bytes 1769480 | tf_op jit(solution)/shard_map/ppermute | solution.py:372
  975.5 320.8 %collective-permute-start.9 = (bf16[192,1536]{1,0:T(8,128)(2,1)}, bf16[192,1536]{1,0:T(8,128)(2,1)}, u32[]{:S(2)}, u32[]{:S(2)}) collective-permute-start(bf16[192,1536]{1,0:T(8,128)(2,1)} %get-tuple-element.120), channel_id=1, source_target_pairs={{8,20},{20,0},{0,12},{9,21},{21,1},{1,13},{10,22},{22,2},{2,14},{1... | collective-permute-start | bytes 1769480 | tf_op jit(solution)/shard_map/ppermute | solution.py:372
  977.0 321.2 %collective-permute-start.10 = (bf16[192,1536]{1,0:T(8,128)(2,1)}, bf16[192,1536]{1,0:T(8,128)(2,1)}, u32[]{:S(2)}, u32[]{:S(2)}) collective-permute-start(bf16[192,1536]{1,0:T(8,128)(2,1)} %get-tuple-element.119), channel_id=1, source_target_pairs={{8,24},{20,4},{0,16},{9,25},{21,5},{1,17},{10,26},{22,6},{2,18},{1... | collective-permute-start | bytes 1769480 | tf_op jit(solution)/shard_map/ppermute | solution.py:372
  978.5 321.6 %collective-permute-start.11 = (bf16[192,1536]{1,0:T(8,128)(2,1)}, bf16[192,1536]{1,0:T(8,128)(2,1)}, u32[]{:S(2)}, u32[]{:S(2)}) collective-permute-start(bf16[192,1536]{1,0:T(8,128)(2,1)} %get-tuple-element.118), channel_id=1, source_target_pairs={{8,28},{20,8},{0,20},{9,29},{21,9},{1,21},{10,30},{22,10},{2,22},{... | collective-permute-start | bytes 1769480 | tf_op jit(solution)/shard_map/ppermute | solution.py:372
  1137.8 187.7 %reduce-scatter.14.cloned.1.call-start = ((), (), s32[]{:S(2)}) async-start(), calls=%async_computation.9 | async-start | bytes 4055040 | tf_op jit(solution)/shard_map/reduce_scatter | solution.py:576
  1255.6 34.8 %copy-start.51 = (bf16[192,1536]{1,0:T(8,128)(2,1)S(1)}, bf16[192,1536]{1,0:T(8,128)(2,1)}, u32[]{:S(2)}) copy-start(bf16[192,1536]{1,0:T(8,128)(2,1)} %get-tuple-element.117) | copy-start | bytes 1769476
  1256.4 36.6 %copy-start.81 = (f32[3,192]{1,0:T(4,128)}, f32[3,192]{1,0:T(4,128)S(1)}, u32[]{:S(2)}) copy-start(f32[3,192]{1,0:T(4,128)S(1)} %convert_reduce_fusion.1) | copy-start | bytes 6916
  1257.0 36.0 %copy-start.50 = (bf16[192,1536]{1,0:T(8,128)(2,1)S(1)}, bf16[192,1536]{1,0:T(8,128)(2,1)}, u32[]{:S(2)}) copy-start(bf16[192,1536]{1,0:T(8,128)(2,1)} %get-tuple-element.116) | copy-start | bytes 1769476
  1290.4 11.7 collective-permute-start.12
  1293.0 25.3 %collective-permute-start.13 = (bf16[192,1536]{1,0:T(8,128)(2,1)S(1)}, bf16[192,1536]{1,0:T(8,128)(2,1)S(1)}, u32[]{:S(2)}, u32[]{:S(2)}) collective-permute-start(bf16[192,1536]{1,0:T(8,128)(2,1)S(1)} %copy-done.50), channel_id=1, source_target_pairs={{8,4},{20,16},{0,28},{9,5},{21,17},{1,29},{10,6},{22,18},{2,30},{1... | collective-permute-start | bytes 1769480 | tf_op jit(solution)/shard_map/ppermute | solution.py:372
  (86 other events, 700.1 us)
Sparse Core Ops, SparseCore 0:
  10.2 135.3 all-gather.2
  147.8 193.4 all-gather.4
  405.2 228.5 reduce-scatter.9
  731.4 215.8 reduce-scatter.11
  970.9 132.9 reduce-scatter.15
  1137.9 28.2 reduce-scatter.17
  1241.3 38.7 reduce-scatter.13
